TPU v7x, 8 devices: a whole 2x2x1 slice. The times are simulated.
8 devices in a mesh: dp: 2 (over z, y), tp: 4 (over x, core).
Axes of the slice: x: 2, y: 2, z: 1, core: 2. Of those that a mesh axis runs over, the one named last changes fastest.
Arguments:
- x_seq: bfloat16 [4, 1024, 8192], P('dp', 'tp'), parts along dimension 0
- ln_gain: bfloat16 [8192], replicated
- w_qkv: bfloat16 [8192, 8, 1280], P(None, 'tp')
- w_out: bfloat16 [8192, 8192], P('tp')
- y_grad: bfloat16 [4, 1024, 8192], P('dp', 'tp'), parts along dimension 0
Outputs:
- output 1: bfloat16 [4, 1024, 8192], P('dp', 'tp'), parts along dimension 0
- output 2: bfloat16 [4, 1024, 8192], P('dp', 'tp'), parts along dimension 0
- output 3: bfloat16 [16384], P('dp'), parts along dimension 0
- output 4: bfloat16 [16384, 8, 1280], P('dp', 'tp'), parts along dimension 0
- output 5: bfloat16 [16384, 8192], P(('dp', 'tp')), parts along dimension 0
There are 2 independent parts. A program takes and returns all parts, laid end to end along the dimension named above; an argument that names none is the same for every part.
All inputs are finite; a program needn't handle non-finite values.
Results may differ from a plain program's by a relative error of at most 0.0165068.
Values are sent between devices in bfloat16 or wider.
A program may use at most 1 GiB of HBM per device.

v0:
```python
import functools
import jax
import jax.numpy as jnp
from jax import lax
from jax.sharding import PartitionSpec as P

CLIP_QKV = 8.0
ROPE_THETA = 500000.0
LN_EPS = 1e-5


def layer_norm(x_f32, gain_f32):
    row_mean = jnp.mean(x_f32, axis=-1, keepdims=True)
    centered = x_f32 - row_mean
    variance = jnp.mean(centered * centered, axis=-1, keepdims=True)
    return (centered * lax.rsqrt(variance + LN_EPS) * gain_f32).astype(jnp.bfloat16)


def rope_tables(positions, head_dim):
    inv_freq = 1.0 / (ROPE_THETA ** (jnp.arange(0, head_dim, 2, dtype=jnp.float32) / head_dim))
    angles = positions.astype(jnp.float32)[:, None] * inv_freq[None, :]
    return jnp.cos(angles), jnp.sin(angles)


def rotate(vec_in, cos_t, sin_t):
    half_dim = vec_in.shape[-1] // 2
    half_lo = vec_in[..., :half_dim]
    half_hi = vec_in[..., half_dim:]
    return jnp.concatenate([half_lo * cos_t - half_hi * sin_t, half_hi * cos_t + half_lo * sin_t], axis=-1)


def attention_core(qkv_clip, head_dim):
    batch_n, seq_len, kv_loc, slot_width = qkv_clip.shape
    groups = slot_width // head_dim - 2
    qkv_slots = qkv_clip.reshape(batch_n, seq_len, kv_loc, groups + 2, head_dim)
    cos_t, sin_t = rope_tables(jnp.arange(seq_len), head_dim)
    query_rot = rotate(qkv_slots[:, :, :, :groups].astype(jnp.float32), cos_t[:, None, None], sin_t[:, None, None]).astype(jnp.bfloat16)
    key_rot = rotate(qkv_slots[:, :, :, groups].astype(jnp.float32), cos_t[:, None], sin_t[:, None]).astype(jnp.bfloat16)
    val_head = qkv_slots[:, :, :, groups + 1]
    scores = jnp.einsum('bqngd,bknd->bngqk', query_rot, key_rot, preferred_element_type=jnp.float32) * head_dim ** -0.5
    causal = jnp.arange(seq_len)[:, None] >= jnp.arange(seq_len)[None, :]
    scores = jnp.where(causal, scores, -1e30)
    attn_prob = jax.nn.softmax(scores, axis=-1).astype(jnp.bfloat16)
    mixed = jnp.einsum('bngqk,bknd->bqngd', attn_prob, val_head, preferred_element_type=jnp.float32).astype(jnp.bfloat16)
    return mixed.reshape(batch_n, seq_len, kv_loc * groups * head_dim)


def solution(mesh):
    def device_step(x_seq, ln_gain, w_qkv, w_out, y_grad):
        kv_loc = w_qkv.shape[1]
        head_dim = (w_qkv.shape[2] - w_out.shape[0] // kv_loc) // 2
        x_f32 = x_seq.astype(jnp.float32)
        h_loc, norm_pullback = jax.vjp(layer_norm, x_f32, ln_gain.astype(jnp.float32))
        h_full = lax.all_gather(h_loc, 'tp', axis=1, tiled=True)
        qkv_raw = jnp.einsum('bsd,dnc->bsnc', h_full, w_qkv, preferred_element_type=jnp.float32).astype(jnp.bfloat16)
        qkv_clip = jnp.minimum(jnp.maximum(qkv_raw, -CLIP_QKV), CLIP_QKV)
        attn_out, core_pullback = jax.vjp(functools.partial(attention_core, head_dim=head_dim), qkv_clip)
        out_part = jnp.einsum('bsk,kd->bsd', attn_out, w_out, preferred_element_type=jnp.float32).astype(jnp.bfloat16)
        out_loc = lax.psum_scatter(out_part, 'tp', scatter_dimension=1, tiled=True)
        y_out = (x_f32 + out_loc.astype(jnp.float32)).astype(jnp.bfloat16)
        grad_full = lax.all_gather(y_grad, 'tp', axis=1, tiled=True)
        wout_grad = jnp.einsum('bsk,bsd->kd', attn_out, grad_full, preferred_element_type=jnp.float32).astype(jnp.bfloat16)
        d_attn = jnp.einsum('bsd,kd->bsk', grad_full, w_out, preferred_element_type=jnp.float32).astype(jnp.bfloat16)
        (d_clip,) = core_pullback(d_attn)
        d_qkv = jnp.where(jnp.abs(qkv_raw) < CLIP_QKV, d_clip, jnp.zeros_like(d_clip))
        wqkv_grad = jnp.einsum('bsd,bsnc->dnc', h_full, d_qkv, preferred_element_type=jnp.float32).astype(jnp.bfloat16)
        dh_part = jnp.einsum('bsnc,dnc->bsd', d_qkv, w_qkv, preferred_element_type=jnp.float32).astype(jnp.bfloat16)
        dh_loc = lax.psum_scatter(dh_part, 'tp', scatter_dimension=1, tiled=True)
        dx_norm, gain_part = norm_pullback(dh_loc)
        x_grad = (y_grad.astype(jnp.float32) + dx_norm).astype(jnp.bfloat16)
        gain_grad = lax.psum(gain_part, 'tp').astype(jnp.bfloat16)
        return y_out, x_grad, gain_grad, wqkv_grad, wout_grad

    specs_in = (P('dp', 'tp', None), P(None), P(None, 'tp', None), P('tp', None), P('dp', 'tp', None))
    specs_out = (P('dp', 'tp', None), P('dp', 'tp', None), P('dp'), P('dp', 'tp', None), P(('dp', 'tp'), None))
    return jax.shard_map(device_step, mesh=mesh, in_specs=specs_in, out_specs=specs_out, check_vma=False)
```

profile of v0, /device:TPU:0, one launch (start us, length us, event | category | flops | bytes accessed | tf_op | source)
XLA Modules:
  0.0 1604.8 jit_solution(7851946452310254463)
XLA Ops:
  7.2 4.6 convert_reduce_fusion
  11.8 5.7 fusion.35
  17.5 0.6 copy-done.20
  18.7 0.6 copy-done.14
  19.3 11.4 fusion.33
  30.7 0.7 all-gather.5.cloned.1.call-update
  32.0 1.3 iota_compare_fusion.1
  33.3 1.3 iota_compare_fusion
  34.6 3.0 multiply_cosine_fusion
  37.7 195.4 %all-gather.3.cloned.1.call-done = bf16[2,1024,8192]{2,1,0:T(8,128)(2,1)} async-done(((bf16[2,256,8192]{2,1,0:T(8,128)(2,1)}), bf16[2,1024,8192]{2,1,0:T(8,128)(2,1)}) %all-gather.3.cloned.1.call-update) | async-done | bytes 33554448 | tf_op jit(solution)/shard_map/all_gather | solution.py:54
  233.0 102.5 %broadcast_clamp_fusion = (bf16[2,1024,2,1280]{3,1,2,0:T(8,128)(2,1)}, bf16[2,1024,2,1280]{3,1,2,0:T(8,128)(2,1)}) fusion(bf16[8192,2,1280]{2,1,0:T(2,128)(2,1)} %param.7, bf16[2,1024,8192]{2,1,0:T(8,128)(2,1)} %all-gather.3.cloned.1.call-done), kind=kOutput, calls=%fused_computation.67 | convolution fusion | flops 85909831680 | bytes 96468992 | tf_op jit(solution)/shard_map/bsd,dnc->bsnc/dot_general | solution.py:55
  335.5 14.4 copy.30
  349.9 1.3 slice.29
  351.2 8.4 slice.32
  359.6 74.3 %all-gather.5.cloned.1.call-done = bf16[2,1024,8192]{2,1,0:T(8,128)(2,1)} async-done(((bf16[2,256,8192]{2,1,0:T(8,128)(2,1)}), bf16[2,1024,8192]{2,1,0:T(8,128)(2,1)}) %all-gather.5.cloned.1.call-update) | async-done | bytes 33554448 | tf_op jit(solution)/shard_map/all_gather | solution.py:61
  433.9 79.7 %fusion.46 = bf16[2,1024,2048]{2,1,0:T(8,128)(2,1)} fusion(bf16[2,1024,8192]{2,1,0:T(8,128)(2,1)} %all-gather.5.cloned.1.call-done, bf16[2048,8192]{1,0:T(8,128)(2,1)} %param.8), kind=kOutput, calls=%fused_computation.63 | convolution fusion | flops 68723671040 | bytes 75497472 | tf_op jit(solution)/shard_map/bsd,kd->bsk/dot_general | solution.py:63
  513.7 11.8 copy.65
  525.5 0.7 copy.74
  526.3 11.3 copy.75
  537.6 11.6 convert_element_type.156
  549.3 0.8 subtract_convert_fusion.1
  550.1 18.1 %subtract_convert_fusion = (bf16[2,1024,2,8,64]{4,1,3,2,0:T(8,128)(2,1)}, bf16[2,1024,2,8,64]{4,1,3,2,0:T(8,128)(2,1)}) fusion(f32[2,1024,2,8,128]{4,1,3,2,0:T(8,128)} %convert_element_type.156, f32[1024,64]{1,0:T(8,128)S(1)} %copy-done.2, f32[1024,64]{1,0:T(8,128)S(1)} %copy-done), kind=kLoop, calls=%fused_computation.57 | loop fusion | flops 16777216 | bytes 25690112 | tf_op jit(solution)/shard_map/convert.4
  568.2 53.6 %fusion.7 = (f32[2,2,8,1024]{3,2,1,0:T(8,128)S(1)}, f32[2,2,1024,1024,8]{3,2,4,1,0:T(8,128)}) fusion(pred[1024,1024]{0,1:T(8,128)(4,1)S(1)} %copy-done.11, bf16[2,1024,2,8,64]{4,1,3,2,0:T(8,128)(2,1)} %get-tuple-element.22, bf16[2,1024,2,8,64]{4,1,3,2,0:T(8,128)(2,1)} %get-tuple-element.21, bf16[2,1024,2,64]{3,1,2,0:T(8,128)(2,1)S(1)} %get-tuple-element.28, ...), kind=kOutput, calls=%fused_computation.12 | convolution fusion | flops 8709439488 | bytes 144834560 | tf_op jit(solution)/shard_map/jvp(bqngd,bknd->bngqk)/dot_general | solution.py:40
  621.8 41.2 %fusion.8 = f32[2,2,8,1024]{3,2,1,0:T(8,128)S(1)} fusion(f32[2,2,1024,1024,8]{3,2,4,1,0:T(8,128)} %get-tuple-element.34, f32[2,2,8,1024]{3,2,1,0:T(8,128)S(1)} %get-tuple-element.33, pred[1024,1024]{0,1:T(8,128)(4,1)S(1)} %copy-done.11), kind=kLoop, calls=%fused_computation.14 | loop fusion | flops 134184960 | bytes 135528448 | tf_op jit(solution)/shard_map/jvp()/reduce_sum | solution.py:43
  663.0 104.3 %fusion.6 = (f32[2,2,8,1024]{3,2,1,0:T(8,128)S(1)}, bf16[2,2,8,1024,1024]{3,4,2,1,0:T(8,128)(2,1)}, bf16[2,2,8,1024,1024]{3,4,2,1,0:T(8,128)(2,1)}) fusion(f32[2,2,1024,1024,8]{3,2,4,1,0:T(8,128)} %get-tuple-element.34, f32[2,2,8,1024]{3,2,1,0:T(8,128)S(1)} %multiply_divide_fusion, f32[2,2,8,1024]{3,2,1,0:T(8,128)S(1)} %get-tuple-element.33, ...), kind=kOutput, calls=%fused_computation.8 | convolution fusion | flops 8925446144 | bytes 279445504 | tf_op jit(solution)/shard_map/transpose(jvp(bngqk,bknd->bqngd))/dot_general | solution.py:44
  767.3 85.5 %fusion.4 = bf16[2,2,1024,1024,8]{3,2,4,1,0:T(8,128)(2,1)} fusion(bf16[2,2,8,1024,1024]{3,4,2,1,0:T(8,128)(2,1)} %get-tuple-element.35, f32[2,2,1024,1024,8]{3,2,4,1,0:T(8,128)} %get-tuple-element.34, f32[2,2,1024,8]{2,3,1,0:T(8,128)S(1)} %bitcast.161, f32[2,2,1024,8]{2,3,1,0:T(8,128)S(1)} %negate_bitcast_fusion, f32[2,2,1024,8]{2,3,1,0:T(8,128)S(1)} %bitcast.160, ...), kind=kLoop, calls=%fused_computation.6 | loop fusion | flops 335544320 | bytes 269877248 | tf_op jit(solution)/shard_map/transpose(jvp())/mul | solution.py:40
  852.9 30.9 %convert_bitcast_fusion.2 = f32[2,1024,2,128]{3,1,2,0:T(8,128)S(1)} fusion(bf16[2,2,1024,1024,8]{3,2,4,1,0:T(8,128)(2,1)} %fusion.4, bf16[2,1024,2,8,64]{4,1,3,2,0:T(8,128)(2,1)} %get-tuple-element.22, bf16[2,1024,2,8,64]{4,1,3,2,0:T(8,128)(2,1)} %get-tuple-element.21), kind=kOutput, calls=%fused_computation.74 | convolution fusion | flops 8607236096 | bytes 77594624 | tf_op jit(solution)/shard_map/transpose(jvp(bqngd,bknd->bngqk))/dot_general | solution.py:40
  883.8 35.5 %convert_bitcast_fusion.1 = f32[2,1024,2,8,128]{4,1,3,2,0:T(8,128)} fusion(bf16[2,2,1024,1024,8]{3,2,4,1,0:T(8,128)(2,1)} %fusion.4, bf16[2,1024,2,64]{3,1,2,0:T(8,128)(2,1)} %copy-done.9, bf16[2,1024,2,64]{3,1,2,0:T(8,128)(2,1)S(1)} %copy-done.8), kind=kOutput, calls=%fused_computation.51 | convolution fusion | flops 8596226048 | bytes 84934656 | tf_op jit(solution)/shard_map/transpose(jvp(bqngd,bknd->bngqk))/dot_general | solution.py:40
  919.3 11.3 fusion.49
  930.6 28.8 %fusion.54 = bf16[2,1024,2,1,128]{4,1,3,2,0:T(8,128)(2,1)} fusion(bf16[2,2,128,8,1024]{4,2,3,1,0:T(8,128)(2,1)} %bitcast.159, bf16[2,2,8,1024,1024]{3,4,2,1,0:T(8,128)(2,1)} %get-tuple-element.18), kind=kOutput, calls=%fused_computation.80 | convolution fusion | flops 8590458880 | bytes 76546048 | tf_op jit(solution)/shard_map/transpose(jvp(bngqk,bknd->bqngd))/dot_general | solution.py:44
  959.4 2.7 multiply_add_fusion.3
  962.1 18.4 %multiply_add_fusion.1 = (f32[2,1024,2,8,64]{4,1,3,2,0:T(8,128)S(1)}, f32[2,1024,2,8,64]{4,1,3,2,0:T(8,128)}) fusion(f32[2,1024,2,8,128]{4,1,3,2,0:T(8,128)} %convert_bitcast_fusion.1, f32[1024,64]{1,0:T(8,128)S(1)} %copy-done.3, f32[1024,64]{1,0:T(8,128)S(1)} %copy-done.1), kind=kLoop, calls=%fused_computation.55 | loop fusion | flops 14680064 | bytes 34078720 | tf_op jit(solution)/shard_map/transpose(jvp())/add_any | solution.py:29
  980.5 0.6 fusion.56
  981.1 8.5 add_convert_fusion.1
  989.6 4.5 pad_add_fusion
  994.1 14.3 copy.44
  1008.4 15.2 copy.45
  1023.6 99.7 %bitcast_convert_fusion.2 = bf16[2,1024,8192]{2,1,0:T(8,128)(2,1)} fusion(bf16[8192,2,1280]{2,1,0:T(2,128)(2,1)} %param.7, bf16[2,1024,2,1280]{3,1,2,0:T(8,128)(2,1)} %copy.45, u8[1024,2,1280]{2,0,1:T(8,128)(4,1)S(1)} %copy-done.12), kind=kOutput, calls=%fused_computation.16 | convolution fusion | flops 85942337536 | bytes 88604672 | tf_op jit(solution)/shard_map/bsnc,dnc->bsd/dot_general | solution.py:67
  1123.5 27.1 %convolution_convert_fusion.1 = bf16[2,2,128,8,1024]{4,2,3,1,0:T(8,128)(2,1)} fusion(bf16[2,2,8,1024,1024]{3,4,2,1,0:T(8,128)(2,1)} %get-tuple-element.18, bf16[2,1024,2,10,128]{1,4,3,2,0:T(8,128)(2,1)} %bitcast.154), kind=kOutput, calls=%fused_computation.62 | convolution fusion | flops 8594128896 | bytes 76546048 | tf_op jit(solution)/shard_map/jvp(bngqk,bknd->bqngd)/dot_general | solution.py:44
  1150.5 78.8 %fusion.25 = bf16[2,1024,8192]{2,1,0:T(8,128)(2,1)} fusion(bf16[2,1024,2048]{1,2,0:T(8,128)(2,1)} %bitcast.156, bf16[2048,8192]{1,0:T(8,128)(2,1)} %param.8), kind=kOutput, calls=%fused_computation.38 | convolution fusion | flops 68736253952 | bytes 75497472 | tf_op jit(solution)/shard_map/bsk,kd->bsd/dot_general | solution.py:58
  1229.3 98.6 %bitcast_convert_fusion = bf16[8192,2,1280]{2,0,1:T(8,128)(2,1)} fusion(bf16[2,1024,8192]{2,1,0:T(8,128)(2,1)} %all-gather.3.cloned.1.call-done, bf16[2,1024,2,1280]{3,1,2,0:T(8,128)(2,1)} %copy.45, u8[1024,2,1280]{2,0,1:T(8,128)(4,1)S(1)} %copy-done.12), kind=kOutput, calls=%fused_computation.13 | convolution fusion | flops 85946531840 | bytes 88604672 | tf_op jit(solution)/shard_map/bsd,bsnc->dnc/dot_general | solution.py:66
  1327.9 75.4 %copy.49 = bf16[8192,2,1280]{2,1,0:T(2,128)(2,1)} copy(bf16[8192,2,1280]{2,0,1:T(8,128)(2,1)} %bitcast_convert_fusion) | data formatting | bytes 83886080
  1403.3 77.0 %bitcast_convert_fusion.1 = bf16[2048,8192]{1,0:T(8,128)(2,1)} fusion(bf16[2,1024,2048]{1,2,0:T(8,128)(2,1)S(1)} %bitcast.157, bf16[2,1024,8192]{2,1,0:T(8,128)(2,1)} %all-gather.5.cloned.1.call-done), kind=kOutput, calls=%fused_computation.15 | convolution fusion | flops 68736253952 | bytes 75497472 | tf_op jit(solution)/shard_map/bsk,bsd->kd/dot_general | solution.py:62
  1480.4 9.2 fusion.36
  1489.6 12.2 fusion.34
  1501.8 12.4 psum.7
  1514.2 64.3 %reduce-scatter.3.cloned.1.call-done = bf16[2,256,8192]{2,1,0:T(8,128)(2,1)} async-done(((bf16[2,1024,8192]{2,1,0:T(8,128)(2,1)}), bf16[2,256,8192]{2,1,0:T(8,128)(2,1)}) %reduce-scatter.3.cloned.1.call-update) | async-done | bytes 8388624 | tf_op jit(solution)/shard_map/reduce_scatter | solution.py:59
  1578.5 19.3 %add_convert_fusion = (bf16[2,256,8192]{2,1,0:T(8,128)(2,1)}, bf16[2,256,8192]{2,1,0:T(8,128)(2,1)}) fusion(bf16[2,256,8192]{2,1,0:T(8,128)(2,1)} %param.9, bf16[2,256,8192]{2,1,0:T(8,128)(2,1)} %param.5, bf16[2,256,8192]{2,1,0:T(8,128)(2,1)} %reduce-scatter.5.cloned.1.call-done, f32[2,256]{1,0:T(2,128)S(1)} %negate_multiply_fusion, ...), kind=kLoop, calls=%fused_computation.52 | loop fusion | flops 62914560 | bytes 50372608 | tf_op jit(solution)/shard_map/convert_element_type | solution.py:70
  (62 shorter events, 1.6 us)
Async XLA Ops:
  7.2 10.9 copy-start.22
  7.2 225.8 %all-gather.3.cloned.1.call-start = ((), (), s32[]{:S(2)}) async-start(), calls=%async_computation.2 | async-start | bytes 41943040 | tf_op jit(solution)/shard_map/all_gather | solution.py:54
  11.8 6.3 copy-start.16
  17.5 0.6 copy-start.20
  18.1 0.6 copy-start.18
  18.7 0.6 copy-start.14
  30.7 403.3 %all-gather.5.cloned.1.call-start = ((), (), s32[]{:S(2)}) async-start(), calls=%async_computation.4 | async-start | bytes 41943040 | tf_op jit(solution)/shard_map/all_gather | solution.py:61
  31.4 1448.9 %reduce-scatter.5.cloned.1.call-start = ((), (), s32[]{:S(2)}) async-start(), calls=%async_computation.5 | async-start | bytes 41943040 | tf_op jit(solution)/shard_map/reduce_scatter | solution.py:68
  537.6 11.6 copy-start
  537.6 11.6 copy-start.2
  550.0 18.1 %copy-start.7 = (bf16[2,1024,2,64]{3,1,2,0:T(8,128)(2,1)}, bf16[2,1024,2,64]{3,1,2,0:T(8,128)(2,1)S(1)}, u32[]{:S(2)}) copy-start(bf16[2,1024,2,64]{3,1,2,0:T(8,128)(2,1)S(1)} %get-tuple-element.27) | copy-start | bytes 1572868
  550.0 18.1 %copy-start.9 = (bf16[2,1024,2,64]{3,1,2,0:T(8,128)(2,1)}, bf16[2,1024,2,64]{3,1,2,0:T(8,128)(2,1)S(1)}, u32[]{:S(2)}) copy-start(bf16[2,1024,2,64]{3,1,2,0:T(8,128)(2,1)S(1)} %get-tuple-element.28) | copy-start | bytes 1572868
  550.0 18.1 %copy-start.11 = (pred[1024,1024]{0,1:T(8,128)(4,1)S(1)}, pred[1024,1024]{0,1:T(8,128)(4,1)}, u32[]{:S(2)}) copy-start(pred[1024,1024]{0,1:T(8,128)(4,1)} %iota_compare_fusion.1) | copy-start | bytes 3145732
  663.0 104.3 %copy-start.10 = (pred[1024,1024]{1,0:T(8,128)(4,1)S(1)}, pred[1024,1024]{1,0:T(8,128)(4,1)}, u32[]{:S(2)}) copy-start(pred[1024,1024]{1,0:T(8,128)(4,1)} %iota_compare_fusion) | copy-start | bytes 3145732
  852.9 31.0 %copy-start.8 = (bf16[2,1024,2,64]{3,1,2,0:T(8,128)(2,1)S(1)}, bf16[2,1024,2,64]{3,1,2,0:T(8,128)(2,1)}, u32[]{:S(2)}) copy-start(bf16[2,1024,2,64]{3,1,2,0:T(8,128)(2,1)} %copy-done.7) | copy-start | bytes 1572868
  930.6 28.8 %copy-start.1 = (f32[1024,64]{1,0:T(8,128)S(1)}, f32[1024,64]{1,0:T(8,128)}, u32[]{:S(2)}) copy-start(f32[1024,64]{1,0:T(8,128)} %get-tuple-element.29) | copy-start | bytes 786436
  930.6 28.8 %copy-start.3 = (f32[1024,64]{1,0:T(8,128)S(1)}, f32[1024,64]{1,0:T(8,128)}, u32[]{:S(2)}) copy-start(f32[1024,64]{1,0:T(8,128)} %get-tuple-element.30) | copy-start | bytes 786436
  962.1 18.4 %copy-start.5 = (f32[2,1024,2,64]{3,1,2,0:T(8,128)S(1)}, f32[2,1024,2,64]{3,1,2,0:T(8,128)}, u32[]{:S(2)}) copy-start(f32[2,1024,2,64]{3,1,2,0:T(8,128)} %get-tuple-element.25) | copy-start | bytes 3145732
  962.1 18.4 %copy-start.6 = (f32[2,1024,2,64]{3,1,2,0:T(8,128)S(1)}, f32[2,1024,2,64]{3,1,2,0:T(8,128)}, u32[]{:S(2)}) copy-start(f32[2,1024,2,64]{3,1,2,0:T(8,128)} %get-tuple-element.26) | copy-start | bytes 3145732
  981.1 8.5 copy-start.13
  994.1 29.5 %copy-start.12 = (u8[1024,2,1280]{2,0,1:T(8,128)(4,1)S(1)}, u8[1024,2,1280]{2,0,1:T(8,128)(4,1)}, u32[]{:S(2)}) copy-start(u8[1024,2,1280]{2,0,1:T(8,128)(4,1)} %fusion.49) | copy-start | bytes 7864324
  1123.4 455.1 %reduce-scatter.3.cloned.1.call-start = ((), (), s32[]{:S(2)}) async-start(), calls=%async_computation.3 | async-start | bytes 41943040 | tf_op jit(solution)/shard_map/reduce_scatter | solution.py:59
  1327.9 75.4 %copy-start.4 = (bf16[2,2,128,8,1024]{4,2,3,1,0:T(8,128)(2,1)S(1)}, bf16[2,2,128,8,1024]{4,2,3,1,0:T(8,128)(2,1)}, u32[]{:S(2)}) copy-start(bf16[2,2,128,8,1024]{4,2,3,1,0:T(8,128)(2,1)} %convolution_convert_fusion.1) | copy-start | bytes 25165828
  1403.3 77.1 %copy-start.15 = (f32[8192]{0:T(1024)S(1)}, f32[8192]{0:T(1024)}, u32[]{:S(2)}) copy-start(f32[8192]{0:T(1024)} %copy-done.14) | copy-start | bytes 98308
  1403.3 77.1 %copy-start.17 = (f32[2,256]{1,0:T(2,128)S(1)}, f32[2,256]{1,0:T(2,128)}, u32[]{:S(2)}) copy-start(f32[2,256]{1,0:T(2,128)} %copy-done.16) | copy-start | bytes 6148
  1480.3 9.3 copy-start.21
  1480.3 9.3 copy-start.19
Sparse Core Ops, SparseCore 0:
  30.8 202.1 all-gather.2
  234.5 199.3 all-gather.4
  1123.5 225.9 reduce-scatter.4
  1351.9 226.5 reduce-scatter.2
where the time goes:
time: 1610 us; the launch traced here: 1600 us
  matrix products  817 us (51%)
  waiting for transfers between devices  335 us (21%)
  other arithmetic  271 us (17%)
  local copies, waits for them, and re-layouts  155 us (10%)
    all_gather x1, waiting for transfers between devices, device_step(): h_full = lax.all_gather(h_loc, 'tp', axis=1, tiled=True)  195 us
    dot_general x3, matrix products, attention_core(): jnp.einsum('bngqk,bknd->bqngd', attn_prob, val_head, preferred_element_ty...  160 us
    dot_general x3, matrix products, attention_core(): jnp.einsum('bqngd,bknd->bngqk', query_rot, key_rot, preferred_element_typ...  120 us
    dot_general x1, matrix products, device_step(): jnp.einsum('bsd,dnc->bsnc', h_full, w_qkv, preferred_element_type=jnp.flo...  102 us
    dot_general x1, matrix products, device_step(): jnp.einsum('bsnc,dnc->bsd', d_qkv, w_qkv, preferred_element_type=jnp.floa...  99.7 us
    dot_general x1, matrix products, device_step(): jnp.einsum('bsd,bsnc->dnc', h_full, d_qkv, preferred_element_type=jnp.flo...  98.6 us
    unnamed x49, local copies, waits for them, and re-layouts  89.2 us
    mul x1, other arithmetic, attention_core(): jnp.einsum('bqngd,bknd->bngqk', query_rot, key_rot, preferred_element_typ...  85.5 us
  transfers between devices with their start and end apart: 4, of which 3 were waited for; matrix products, arithmetic and copies ran while one was open for 32% of the time, Pallas kernels for 0%

commit v1 on v0

v1 whole, which is shorter than its diff:
```python
import functools
import jax
import jax.numpy as jnp
from jax import lax
from jax.experimental import pallas as pl
from jax.experimental.pallas import tpu as pltpu
from jax.sharding import PartitionSpec as P

CLIP_QKV = 8.0
ROPE_THETA = 500000.0
LN_EPS = 1e-5
LOG2E = 1.4426950408889634
QBLK = 256
NT = (((1,), (1,)), ((), ()))
NN = (((1,), (0,)), ((), ()))


def dot32(a, b, dims):
    return lax.dot_general(a, b, dims, preferred_element_type=jnp.float32)


def ln_stats(x):
    row_mean = jnp.mean(x, axis=-1, keepdims=True)
    centered = x - row_mean
    variance = jnp.mean(centered * centered, axis=-1, keepdims=True)
    rstd = lax.rsqrt(variance + LN_EPS)
    return centered * rstd, rstd


def ln_fwd_kernel(x_ref, gain_ref, h_ref):
    normed, _ = ln_stats(x_ref[0].astype(jnp.float32))
    h_ref[...] = (normed * gain_ref[...].astype(jnp.float32)).astype(jnp.bfloat16)


def ln_bwd_kernel(dh_ref, x_ref, dy_ref, gain_ref, *refs):
    dx_ref, dgain_ref = refs[-2:]
    normed, rstd = ln_stats(x_ref[0].astype(jnp.float32))
    d_h = dh_ref[...].astype(jnp.float32)
    d_gain = jnp.sum(d_h * normed, axis=0, keepdims=True)
    d_normed = d_h * gain_ref[...].astype(jnp.float32)
    shift = jnp.mean(d_normed, axis=-1, keepdims=True)
    slope = jnp.mean(d_normed * normed, axis=-1, keepdims=True)
    d_x = rstd * (d_normed - shift - normed * slope)
    dx_ref[0] = (dy_ref[0].astype(jnp.float32) + d_x).astype(jnp.bfloat16)

    @pl.when(pl.program_id(0) == 0)
    def _():
        dgain_ref[...] = d_gain

    @pl.when(pl.program_id(0) > 0)
    def _():
        dgain_ref[...] += d_gain


def residual_kernel(o_ref, x_ref, *refs):
    y_ref = refs[-1]
    y_ref[0] = (x_ref[0].astype(jnp.float32) + o_ref[...].astype(jnp.float32)).astype(jnp.bfloat16)


def interleave_kernel(in_ref, out_ref):
    for n in range(in_ref.shape[0]):
        out_ref[:, n, :] = in_ref[n]


def rope_tables(seq_len, head_dim):
    inv_freq = 1.0 / (ROPE_THETA ** (jnp.arange(0, head_dim, 2, dtype=jnp.float32) / head_dim))
    angles = jnp.arange(seq_len, dtype=jnp.float32)[:, None] * inv_freq[None, :]
    cos_t, sin_t = jnp.cos(angles), jnp.sin(angles)
    return jnp.concatenate([cos_t, cos_t], axis=-1), jnp.concatenate([-sin_t, sin_t], axis=-1)


def clip(v):
    return jnp.minimum(jnp.maximum(v, -CLIP_QKV), CLIP_QKV)


def rope(v_f32, cos_t, sin_t):
    return v_f32 * cos_t + pltpu.roll(v_f32, v_f32.shape[-1] // 2, 1) * sin_t


def unrope(v_f32, cos_t, sin_t):
    return v_f32 * cos_t - pltpu.roll(v_f32, v_f32.shape[-1] // 2, 1) * sin_t


def masked_tail(s, fill):
    top, tail = s[:-QBLK], s[-QBLK:]
    rows = lax.broadcasted_iota(jnp.int32, tail.shape, 0)
    cols = lax.broadcasted_iota(jnp.int32, tail.shape, 1)
    tail = jnp.where(rows <= cols, tail, fill)
    return tail if s.shape[0] == QBLK else jnp.concatenate([top, tail], axis=0)


def attn_fwd_kernel(groups, dim, qkv_ref, cos_ref, sin_ref, out_ref, lse_ref, k_scr, vt_scr):
    head = pl.program_id(1)
    seq = qkv_ref.shape[1]

    @pl.when(head == 0)
    def _():
        k_in = clip(qkv_ref[0, :, groups * dim:(groups + 1) * dim].astype(jnp.float32))
        k_scr[...] = rope(k_in, cos_ref[...], sin_ref[...]).astype(jnp.bfloat16)
        v_in = clip(qkv_ref[0, :, (groups + 1) * dim:(groups + 2) * dim].astype(jnp.float32))
        vt_scr[...] = v_in.T.astype(jnp.bfloat16)

    col = pl.ds(pl.multiple_of(head * dim, dim), dim)
    scale = LOG2E * dim ** -0.5
    for i in range(seq // QBLK):
        rows = slice(i * QBLK, (i + 1) * QBLK)
        kend = (i + 1) * QBLK
        q_in = clip(qkv_ref[0, rows, col].astype(jnp.float32))
        q_rot = rope(q_in, cos_ref[rows, :], sin_ref[rows, :]).astype(jnp.bfloat16)
        s = dot32(k_scr[:kend, :], q_rot, NT) * scale
        s = masked_tail(s, -1e30)
        top = jnp.max(s, axis=0, keepdims=True)
        e = jnp.exp2(s - top)
        total = jnp.sum(e, axis=0, keepdims=True)
        prob = (e * (1.0 / total)).astype(jnp.bfloat16)
        o_t = dot32(vt_scr[:, :kend], prob, NN)
        out_ref[rows, col] = o_t.T.astype(jnp.bfloat16)
        lse_ref[0, pl.ds(head, 1), rows] = top + jnp.log2(total)


def attn_bwd_kernel(groups, dim, qkv_ref, do_ref, lse_ref, cos_ref, sin_ref, dqkv_ref,
                    k_scr, kt_scr, v_scr, dk_scr, dv_scr):
    head = pl.program_id(1)
    seq = qkv_ref.shape[1]
    kcol = slice(groups * dim, (groups + 1) * dim)
    vcol = slice((groups + 1) * dim, (groups + 2) * dim)

    @pl.when(head == 0)
    def _():
        k_in = clip(qkv_ref[0, :, kcol].astype(jnp.float32))
        k_rot = rope(k_in, cos_ref[...], sin_ref[...])
        k_scr[...] = k_rot.astype(jnp.bfloat16)
        kt_scr[...] = k_rot.T.astype(jnp.bfloat16)
        v_scr[...] = clip(qkv_ref[0, :, vcol].astype(jnp.float32)).astype(jnp.bfloat16)
        dk_scr[...] = jnp.zeros_like(dk_scr)
        dv_scr[...] = jnp.zeros_like(dv_scr)

    col = pl.ds(pl.multiple_of(head * dim, dim), dim)
    scale = dim ** -0.5
    for i in range(seq // QBLK):
        rows = slice(i * QBLK, (i + 1) * QBLK)
        kend = (i + 1) * QBLK
        q_raw = qkv_ref[0, rows, col].astype(jnp.float32)
        q_rot = rope(clip(q_raw), cos_ref[rows, :], sin_ref[rows, :]).astype(jnp.bfloat16)
        d_o = do_ref[rows, col]
        s = dot32(k_scr[:kend, :], q_rot, NT) * (LOG2E * scale) - lse_ref[0, pl.ds(head, 1), rows]
        p = jnp.exp2(masked_tail(s, -1e30))
        dv_scr[:kend, :] += dot32(p.astype(jnp.bfloat16), d_o, NN)
        dp = dot32(v_scr[:kend, :], d_o, NT).astype(jnp.bfloat16).astype(jnp.float32)
        t = p * dp
        delta = jnp.sum(t, axis=0, keepdims=True)
        ds = (t - p * delta).astype(jnp.bfloat16)
        dk_scr[:kend, :] += dot32(ds, q_rot, NN)
        dq = (dot32(kt_scr[:, :kend], ds, NN) * scale).T.astype(jnp.bfloat16).astype(jnp.float32)
        dq = unrope(dq, cos_ref[rows, :], sin_ref[rows, :])
        dqkv_ref[0, rows, col] = jnp.where(jnp.abs(q_raw) < CLIP_QKV, dq, 0.0).astype(jnp.bfloat16)

    @pl.when(head == groups - 1)
    def _():
        k_raw = qkv_ref[0, :, kcol].astype(jnp.float32)
        v_raw = qkv_ref[0, :, vcol].astype(jnp.float32)
        dk = (dk_scr[...] * scale).astype(jnp.bfloat16).astype(jnp.float32)
        dk = unrope(dk, cos_ref[...], sin_ref[...])
        dqkv_ref[0, :, kcol] = jnp.where(jnp.abs(k_raw) < CLIP_QKV, dk, 0.0).astype(jnp.bfloat16)
        dqkv_ref[0, :, vcol] = jnp.where(jnp.abs(v_raw) < CLIP_QKV, dv_scr[...], 0.0).astype(jnp.bfloat16)


def attn_cost(kv_loc, groups, seq, dim, dots):
    flops = dots * 2 * kv_loc * groups * seq * seq * dim
    return pl.CostEstimate(flops=flops, bytes_accessed=2 * kv_loc * seq * dim * (2 * groups + 2) * 2,
                           transcendentals=kv_loc * groups * seq * seq // 2)


def attn_fwd(qkv, cos_t, sin_t, dim):
    kv_loc, seq, width = qkv.shape
    groups = width // dim - 2
    table = pl.BlockSpec((seq, dim), lambda n, h: (0, 0))
    return pl.pallas_call(
        functools.partial(attn_fwd_kernel, groups, dim),
        grid=(kv_loc, groups),
        in_specs=[pl.BlockSpec((1, seq, width), lambda n, h: (n, 0, 0)), table, table],
        out_specs=[pl.BlockSpec((seq, groups * dim), lambda n, h: (0, n)),
                   pl.BlockSpec((1, groups, seq), lambda n, h: (n, 0, 0))],
        out_shape=[jax.ShapeDtypeStruct((seq, kv_loc * groups * dim), jnp.bfloat16),
                   jax.ShapeDtypeStruct((kv_loc, groups, seq), jnp.float32)],
        scratch_shapes=[pltpu.VMEM((seq, dim), jnp.bfloat16), pltpu.VMEM((dim, seq), jnp.bfloat16)],
        compiler_params=pltpu.CompilerParams(dimension_semantics=("arbitrary", "arbitrary"),
                                             vmem_limit_bytes=48 * 2 ** 20),
        cost_estimate=attn_cost(kv_loc, groups, seq, dim, 4),
        name="attn_fwd",
    )(qkv, cos_t, sin_t)


def attn_bwd(qkv, d_out, lse, cos_t, sin_t, dim):
    kv_loc, seq, width = qkv.shape
    groups = width // dim - 2
    table = pl.BlockSpec((seq, dim), lambda n, h: (0, 0))
    wide = pl.BlockSpec((1, seq, width), lambda n, h: (n, 0, 0))
    return pl.pallas_call(
        functools.partial(attn_bwd_kernel, groups, dim),
        grid=(kv_loc, groups),
        in_specs=[wide, pl.BlockSpec((seq, groups * dim), lambda n, h: (0, n)),
                  pl.BlockSpec((1, groups, seq), lambda n, h: (n, 0, 0)), table, table],
        out_specs=wide,
        out_shape=jax.ShapeDtypeStruct(qkv.shape, jnp.bfloat16),
        scratch_shapes=[pltpu.VMEM((seq, dim), jnp.bfloat16), pltpu.VMEM((dim, seq), jnp.bfloat16),
                        pltpu.VMEM((seq, dim), jnp.bfloat16), pltpu.VMEM((seq, dim), jnp.float32),
                        pltpu.VMEM((seq, dim), jnp.float32)],
        compiler_params=pltpu.CompilerParams(dimension_semantics=("arbitrary", "arbitrary"),
                                             vmem_limit_bytes=48 * 2 ** 20),
        cost_estimate=attn_cost(kv_loc, groups, seq, dim, 8),
        name="attn_bwd",
    )(qkv, d_out, lse, cos_t, sin_t)


def row_call(body, rows, b, flat_in, full_in, extra_in, prev, extra_out):
    tokens, width = full_in[0].shape[1:]
    flat = pl.BlockSpec((rows, width), lambda r: (r, 0))
    full = pl.BlockSpec((1, rows, width), lambda r: (b, r, 0))
    wide = pl.BlockSpec((1, width), lambda r: (0, 0))
    args = [*flat_in, *full_in, *extra_in] + ([] if prev is None else [prev])
    specs = [flat] * len(flat_in) + [full] * len(full_in) + [wide] * len(extra_in)
    if prev is not None:
        specs.append(pl.BlockSpec(memory_space=pl.ANY))
    out_spec = flat if prev is None and not flat_in else full
    out_shape = (tokens, width) if prev is None and not flat_in else full_in[0].shape
    out_shape = [jax.ShapeDtypeStruct(out_shape, jnp.bfloat16)]
    out_shape += [jax.ShapeDtypeStruct((1, width), jnp.float32)] * extra_out
    return pl.pallas_call(
        body, grid=(tokens // rows,), in_specs=specs, out_specs=[out_spec] + [wide] * extra_out, out_shape=out_shape,
        input_output_aliases={} if prev is None else {len(args) - 1: 0},
        compiler_params=pltpu.CompilerParams(dimension_semantics=("arbitrary",), vmem_limit_bytes=40 * 2 ** 20),
        cost_estimate=pl.CostEstimate(flops=40 * tokens * width, bytes_accessed=2 * len(args) * tokens * width,
                                      transcendentals=0),
    )(*args)


def interleave(grad):
    kv_loc, rows, width = grad.shape
    block = 256
    return pl.pallas_call(
        interleave_kernel, grid=(rows // block,),
        in_specs=[pl.BlockSpec((kv_loc, block, width), lambda r: (0, r, 0))],
        out_specs=pl.BlockSpec((block, kv_loc, width), lambda r: (r, 0, 0)),
        out_shape=jax.ShapeDtypeStruct((rows, kv_loc, width), jnp.bfloat16),
        compiler_params=pltpu.CompilerParams(dimension_semantics=("arbitrary",)),
        cost_estimate=pl.CostEstimate(flops=64 * grad.size, bytes_accessed=4 * grad.size, transcendentals=0),
        name="interleave",
    )(grad)


def ein(spec, a, b):
    return jnp.einsum(spec, a, b, preferred_element_type=jnp.float32).astype(jnp.bfloat16)


def solution(mesh):
    def device_step(x_seq, ln_gain, w_qkv, w_out, y_grad):
        batch = x_seq.shape[0]
        kv_loc = w_qkv.shape[1]
        dim = (w_qkv.shape[2] - w_out.shape[0] // kv_loc) // 2
        gain = ln_gain.reshape(1, -1)
        cos_t, sin_t = rope_tables(x_seq.shape[1] * lax.axis_size('tp'), dim)

        def gather(v):
            return lax.all_gather(v, 'tp', axis=0, tiled=True)

        def scatter(v):
            return lax.psum_scatter(v, 'tp', scatter_dimension=0, tiled=True)

        h_full, g_full, qkv, attn, lse, d_qkv, outs, dhs = [], [], [], [], [], [], [], []
        for b in range(batch):
            (h_loc,) = row_call(ln_fwd_kernel, 32, b, [], [x_seq], [gain], None, 0)
            h_full.append(gather(h_loc))
        for b in range(batch):
            g_full.append(gather(y_grad[b]))
        for b in range(batch):
            qkv.append(ein('sd,dnc->nsc', h_full[b], w_qkv))
            a_b, lse_b = attn_fwd(qkv[b], cos_t, sin_t, dim)
            attn.append(a_b)
            lse.append(lse_b)
            outs.append(scatter(ein('sk,kd->sd', a_b, w_out)))
        for b in range(batch):
            d_attn = ein('sd,kd->sk', g_full[b], w_out)
            d_qkv.append(attn_bwd(qkv[b], d_attn, lse[b], cos_t, sin_t, dim))
            dhs.append(scatter(ein('nsc,dnc->sd', d_qkv[b], w_qkv)))
        h_all, g_all = jnp.concatenate(h_full, 0), jnp.concatenate(g_full, 0)
        wout_grad = ein('sk,sd->kd', jnp.concatenate(attn, 0), g_all)
        wqkv_grad = interleave(ein('sd,nsc->ndc', h_all, jnp.concatenate(d_qkv, 1)))
        y_out, x_grad, gain_part = None, None, 0.0
        for b in range(batch):
            x_grad, gain_b = row_call(ln_bwd_kernel, 32, b, [dhs[b]], [x_seq, y_grad], [gain], x_grad, 1)
            gain_part = gain_part + gain_b[0]
        gain_grad = lax.psum(gain_part, 'tp').astype(jnp.bfloat16)
        for b in range(batch):
            (y_out,) = row_call(residual_kernel, 64, b, [outs[b]], [x_seq], [], y_out, 0)
        return y_out, x_grad, gain_grad, wqkv_grad, wout_grad

    specs_in = (P('dp', 'tp', None), P(None), P(None, 'tp', None), P('tp', None), P('dp', 'tp', None))
    specs_out = (P('dp', 'tp', None), P('dp', 'tp', None), P('dp'), P('dp', 'tp', None), P(('dp', 'tp'), None))
    return jax.shard_map(device_step, mesh=mesh, in_specs=specs_in, out_specs=specs_out, check_vma=False)
```

time: 1610 us -> 1030 us (0.64)
  other arithmetic: 271 us -> 2.35 us
  Pallas kernels: 0 us -> 264 us
  matrix products: 817 us -> 577 us
  waiting for transfers between devices: 335 us -> 97 us
  local copies, waits for them, and re-layouts: 155 us -> 49.9 us
    pallas_call x0 -> x11, Pallas kernels: none -> 264 us  [the longest x2 103 us: attn_bwd(): pl.pallas_call(functools.partial(attn_bwd_kernel, groups, dim), grid=(kv_...]
    dot_general x12 -> x10, matrix products: 817 us -> 577 us  [ein(): jnp.einsum(spec, a, b, preferred_element_type=jnp.float32)]
    all_gather x2 -> x4, waiting for transfers between devices: 270 us -> 96.3 us  [gather(): return lax.all_gather(v, 'tp', axis=0, tiled=True)]
    mul x1 -> x0, other arithmetic: 85.5 us -> none  [attention_core(): jnp.einsum('bqngd,bknd->bngqk', query_rot, key_rot, preferred_element_typ...]
    reduce_sum x5 -> x0, other arithmetic: 72.8 us -> none  [the longest x1 41.2 us: attention_core(): attn_prob = jax.nn.softmax(scores, axis=-1).astype(jnp.bfloat16)]
    reduce_scatter x2 -> x4, waiting for transfers between devices: 64.3 us -> 0.03 us  [scatter(): return lax.psum_scatter(v, 'tp', scatter_dimension=0, tiled=True)]
    convert_element_type x7 -> x0, other arithmetic: 51 us -> none  [the longest x2 20.1 us: attention_core(): qkv_slots[:, :, :, :groups].astype(jnp.float32)]
    unnamed x49 -> x32, local copies, waits for them, and re-layouts: 89.2 us -> 43.2 us
  transfers between devices with their start and end apart: 4 -> 8, of which waited for: 3 -> 2; matrix products, arithmetic and copies ran while one was open for 32% -> 58% of each run, Pallas kernels for 0% -> 25%
where the time goes in v1:
time: 1030 us; the launch traced here: 1020 us
  matrix products  577 us (56%)
  Pallas kernels  264 us (26%)
  waiting for transfers between devices  97 us (9%)
  local copies, waits for them, and re-layouts  49.9 us (5%)
  between operations  14.7 us (1%)
  blocking collectives  11.8 us (1%)
    dot_general x10, matrix products, ein(): jnp.einsum(spec, a, b, preferred_element_type=jnp.float32)  577 us
    pallas_call x2, Pallas kernels, attn_bwd(): pl.pallas_call(functools.partial(attn_bwd_kernel, groups, dim), grid=(kv_...  103 us
    all_gather x4, waiting for transfers between devices, gather(): return lax.all_gather(v, 'tp', axis=0, tiled=True)  96.3 us
    pallas_call x2, Pallas kernels, attn_fwd(): pl.pallas_call(functools.partial(attn_fwd_kernel, groups, dim), grid=(kv_...  75.3 us
    pallas_call x1, Pallas kernels, interleave(): pl.pallas_call(interleave_kernel, grid=(rows // block,), in_specs=[pl.Blo...  46.4 us
    unnamed x32, local copies, waits for them, and re-layouts  43.2 us
    pallas_call x6, Pallas kernels, row_call(): pl.pallas_call(body, grid=(tokens // rows,), in_specs=specs, out_specs=[o...  39.6 us
  transfers between devices with their start and end apart: 8, of which 2 were waited for; matrix products, arithmetic and copies ran while one was open for 58% of the time, Pallas kernels for 25%

profile of v1, /device:TPU:0, one launch (start us, length us, event | category | flops | bytes accessed | tf_op | source)
XLA Modules:
  0.0 1016.8 jit_solution(9107560415362529518)
XLA Ops:
  7.2 0.7 reshape.20.gain_ref
  8.0 3.4 copy-done
  11.3 4.5 shard_map.93
  15.8 2.0 copy-done.7
  17.9 6.0 fusion.57
  23.9 0.0 all-gather.7.cloned.1.call-start
  24.0 4.7 copy-done.1
  28.7 4.5 shard_map.92
  33.2 2.0 copy-done.6
  35.3 0.5 all-gather.11.cloned.1.call-update
  35.9 2.0 fusion.52
  37.9 0.3 pad_maximum_fusion
  38.2 85.7 %all-gather.9.cloned.1.call-done = bf16[1024,8192]{1,0:T(8,128)(2,1)} async-done(((bf16[256,8192]{1,0:T(8,128)(2,1)}), bf16[1024,8192]{1,0:T(8,128)(2,1)}) %all-gather.9.cloned.1.call-update) | async-done | bytes 16777232 | tf_op jit(solution)/shard_map/all_gather | solution.py:265
  123.9 55.1 %fusion.40.qkv_ref = bf16[2,1024,1280]{2,1,0:T(8,128)(2,1)} fusion(bf16[8192,2,1280]{2,1,0:T(2,128)(2,1)} %param.7, bf16[1024,8192]{1,0:T(8,128)(2,1)} %all-gather.9.cloned.1.call-done), kind=kOutput, calls=%fused_computation.32 | convolution fusion | flops 42952294400 | bytes 63963136 | tf_op jit(solution)/shard_map/sd,dnc->nsc/dot_general | solution.py:253
  179.0 37.6 %attn_fwd.3 = (bf16[1024,2048]{1,0:T(8,128)(2,1)S(1)}, f32[2,8,1024]{2,1,0:T(8,128)S(1)}) custom-call(bf16[2,1024,1280]{2,1,0:T(8,128)(2,1)} %fusion.40.qkv_ref, f32[1024,128]{1,0:T(8,128)S(1)} %get-tuple-element.26.cos_ref, f32[1024,128]{1,0:T(8,128)S(1)} %get-tuple-element.27.sin_ref), custom_call_target="tpu_custom_call" | custom-call | flops 17179869184 | bytes 18874368 | tf_op jit(solution)/shard_map/attn_fwd/pallas_call | solution.py:178
  216.7 1.9 copy-done.12
  218.6 10.6 %all-gather.13.cloned.1.call-done = bf16[1,1024,8192]{2,1,0:T(8,128)(2,1)} async-done(((bf16[1,256,8192]{2,1,0:T(8,128)(2,1)}), bf16[1,1024,8192]{2,1,0:T(8,128)(2,1)}) %all-gather.13.cloned.1.call-update) | async-done | bytes 16777232 | tf_op jit(solution)/shard_map/all_gather | solution.py:265
  229.2 46.6 %convolution_convert_fusion.3.do_ref = bf16[1024,2048]{1,0:T(8,128)(2,1)} fusion(bf16[2048,8192]{1,0:T(8,128)(2,1)} %param.8, bf16[1,1024,8192]{2,1,0:T(8,128)(2,1)} %all-gather.13.cloned.1.call-done), kind=kOutput, calls=%fused_computation.34 | convolution fusion | flops 34361835520 | bytes 54525952 | tf_op jit(solution)/shard_map/sd,kd->sk/dot_general | solution.py:253
  275.8 2.3 copy-done.15
  278.0 51.4 %attn_bwd.3 = bf16[2,1024,1280]{2,1,0:T(8,128)(2,1)} custom-call(bf16[2,1024,1280]{2,1,0:T(8,128)(2,1)} %fusion.40.qkv_ref, bf16[1024,2048]{1,0:T(8,128)(2,1)S(1)} %copy-done.15, f32[2,8,1024]{2,1,0:T(8,128)S(1)} %get-tuple-element.16.lse_ref, f32[1024,128]{1,0:T(8,128)S(1)} %get-tuple-element.26.cos_ref, f32[1024,128]{1,0:T(8,128)S(1)} %get-tuple-element.27.sin_ref), custom_call_target="tpu_custom_call" | custom-call | flops 34359738368 | bytes 18874368 | tf_op jit(solution)/shard_map/attn_bwd/pallas_call | solution.py:199
  329.4 62.2 %bitcast_convert_fusion = bf16[1024,8192]{1,0:T(8,128)(2,1)} fusion(bf16[2,1024,1280]{2,1,0:T(8,128)(2,1)} %attn_bwd.3, bf16[8192,2,1280]{2,1,0:T(2,128)(2,1)} %param.7), kind=kOutput, calls=%fused_computation.9 | convolution fusion | flops 42958061568 | bytes 63963136 | tf_op jit(solution)/shard_map/nsc,dnc->sd/dot_general | solution.py:253
  391.7 0.0 reduce-scatter.9.cloned.1.call-start
  391.8 53.6 %fusion.45.qkv_ref = bf16[2,1024,1280]{2,1,0:T(8,128)(2,1)} fusion(bf16[8192,2,1280]{2,1,0:T(2,128)(2,1)} %param.7, bf16[1024,8192]{1,0:T(8,128)(2,1)} %all-gather.7.cloned.1.call-done), kind=kOutput, calls=%fused_computation.33 | convolution fusion | flops 42952294400 | bytes 63963136 | tf_op jit(solution)/shard_map/sd,dnc->nsc/dot_general | solution.py:253
  445.4 37.7 %attn_fwd.2 = (bf16[1024,2048]{1,0:T(8,128)(2,1)S(1)}, f32[2,8,1024]{2,1,0:T(8,128)S(1)}) custom-call(bf16[2,1024,1280]{2,1,0:T(8,128)(2,1)} %fusion.45.qkv_ref, f32[1024,128]{1,0:T(8,128)S(1)} %get-tuple-element.26.cos_ref, f32[1024,128]{1,0:T(8,128)S(1)} %get-tuple-element.27.sin_ref), custom_call_target="tpu_custom_call" | custom-call | flops 17179869184 | bytes 18874368 | tf_op jit(solution)/shard_map/attn_fwd/pallas_call | solution.py:178
  483.1 1.9 copy-done.13
  485.0 45.0 %convolution_convert_fusion.4.do_ref = bf16[1024,2048]{1,0:T(8,128)(2,1)} fusion(bf16[2048,8192]{1,0:T(8,128)(2,1)} %param.8, bf16[1,1024,8192]{2,1,0:T(8,128)(2,1)} %all-gather.11.cloned.1.call-done), kind=kOutput, calls=%fused_computation.35 | convolution fusion | flops 34361835520 | bytes 54525952 | tf_op jit(solution)/shard_map/sd,kd->sk/dot_general | solution.py:253
  530.0 2.2 copy-done.14
  532.2 51.5 %attn_bwd.2 = bf16[2,1024,1280]{2,1,0:T(8,128)(2,1)} custom-call(bf16[2,1024,1280]{2,1,0:T(8,128)(2,1)} %fusion.45.qkv_ref, bf16[1024,2048]{1,0:T(8,128)(2,1)S(1)} %copy-done.14, f32[2,8,1024]{2,1,0:T(8,128)S(1)} %get-tuple-element.15.lse_ref, f32[1024,128]{1,0:T(8,128)S(1)} %get-tuple-element.26.cos_ref, f32[1024,128]{1,0:T(8,128)S(1)} %get-tuple-element.27.sin_ref), custom_call_target="tpu_custom_call" | custom-call | flops 34359738368 | bytes 18874368 | tf_op jit(solution)/shard_map/attn_bwd/pallas_call | solution.py:199
  583.7 51.7 %bitcast_convert_fusion.1 = bf16[1024,8192]{1,0:T(8,128)(2,1)} fusion(bf16[2,1024,1280]{2,1,0:T(8,128)(2,1)} %attn_bwd.2, bf16[8192,2,1280]{2,1,0:T(2,128)(2,1)} %param.7), kind=kOutput, calls=%fused_computation.10 | convolution fusion | flops 42958061568 | bytes 63963136 | tf_op jit(solution)/shard_map/nsc,dnc->sd/dot_general | solution.py:253
  635.4 0.0 reduce-scatter.7.cloned.1.call-start
  635.4 43.0 %convolution_convert_fusion.1 = bf16[1024,8192]{1,0:T(8,128)(2,1)} fusion(bf16[1024,2048]{1,0:T(8,128)(2,1)} %copy-done.12, bf16[2048,8192]{1,0:T(8,128)(2,1)} %param.8), kind=kOutput, calls=%fused_computation.22 | convolution fusion | flops 34368126976 | bytes 54525952 | tf_op jit(solution)/shard_map/sk,kd->sd/dot_general | solution.py:253
  678.5 42.5 %convolution_convert_fusion.2 = bf16[1024,8192]{1,0:T(8,128)(2,1)} fusion(bf16[1024,2048]{1,0:T(8,128)(2,1)} %copy-done.13, bf16[2048,8192]{1,0:T(8,128)(2,1)} %param.8), kind=kOutput, calls=%fused_computation.23 | convolution fusion | flops 34368126976 | bytes 54525952 | tf_op jit(solution)/shard_map/sk,kd->sd/dot_general | solution.py:253
  721.0 98.0 %fusion.in_ref = bf16[2,8192,1280]{2,1,0:T(8,128)(2,1)} fusion(bf16[1024,8192]{1,0:T(8,128)(2,1)} %all-gather.7.cloned.1.call-done, bf16[1024,8192]{1,0:T(8,128)(2,1)} %all-gather.9.cloned.1.call-done, bf16[2,1024,1280]{2,1,0:T(8,128)(2,1)} %attn_bwd.2, bf16[2,1024,1280]{2,1,0:T(8,128)(2,1)} %attn_bwd.3), kind=kOutput, calls=%fused_computation.1 | convolution fusion | flops 86008397824 | bytes 85983232 | tf_op jit(solution)/shard_map/sd,nsc->ndc/dot_general | solution.py:253
  819.1 46.4 %interleave.1 = bf16[8192,2,1280]{2,1,0:T(2,128)(2,1)} custom-call(bf16[2,8192,1280]{2,1,0:T(8,128)(2,1)} %fusion.in_ref), custom_call_target="tpu_custom_call" | custom-call | flops 1342177280 | bytes 83886080 | tf_op jit(solution)/shard_map/interleave/pallas_call | solution.py:241
  865.4 79.0 %fusion.7 = bf16[2048,8192]{1,0:T(8,128)(2,1)} fusion(bf16[1024,8192]{1,0:T(8,128)(2,1)} %bitcast.49, bf16[1024,8192]{1,0:T(8,128)(2,1)} %bitcast.48, bf16[1024,2048]{1,0:T(8,128)(2,1)} %copy-done.13, bf16[1024,2048]{1,0:T(8,128)(2,1)} %copy-done.12), kind=kOutput, calls=%fused_computation.11 | convolution fusion | flops 68820140032 | bytes 75497472 | tf_op jit(solution)/shard_map/sk,sd->kd/dot_general | solution.py:253
  944.4 3.4 copy-done.2
  947.8 2.4 copy-done.8
  950.2 12.5 %shard_map.96 = (bf16[2,256,8192]{2,1,0:T(8,128)(2,1)}, f32[1,8192]{1,0:T(1,128)S(1)}) custom-call(bf16[256,8192]{1,0:T(8,128)(2,1)S(1)} %copy-done.8, bf16[2,256,8192]{2,1,0:T(8,128)(2,1)S(1)} %copy-done.2, bf16[2,256,8192]{2,1,0:T(8,128)(2,1)} %dy_ref.3, bf16[1,8192]{1,0:T(2,128)(2,1)S(1)} %reshape.20.gain_ref), custom_call_target="tpu_custom_call" | custom-call | flops 83886080 | bytes 16777216 | tf_op jit(solution)/shard_map/pallas_call | solution.py:229
  962.7 3.6 copy-done.3
  966.3 2.2 copy-done.11
  968.5 12.5 %shard_map.97 = (bf16[2,256,8192]{2,1,0:T(8,128)(2,1)}, f32[1,8192]{1,0:T(1,128)S(1)}) custom-call(bf16[256,8192]{1,0:T(8,128)(2,1)S(1)} %copy-done.11, bf16[2,256,8192]{2,1,0:T(8,128)(2,1)S(1)} %copy-done.3, bf16[2,256,8192]{2,1,0:T(8,128)(2,1)} %dy_ref.3, bf16[1,8192]{1,0:T(2,128)(2,1)S(1)} %reshape.20.gain_ref, ...), custom_call_target="tpu_custom_call", output_to_operand_aliasing={{0}: (4, {})} | custom-call | flops 83886080 | bytes 20971520 | tf_op jit(solution)/shard_map/pallas_call | solution.py:229
  981.1 3.5 copy-done.4
  984.6 2.2 copy-done.9
  986.8 2.8 shard_map.94.refs_0_
  989.5 11.8 %psum.7 = bf16[8192]{0:T(1024)(128)(2,1)} all-reduce(f32[8192]{0:T(1024)S(1)} %bitcast.47), channel_id=1, replica_groups=mesh['dp'=2,'tp'=4] {'tp'}, use_global_device_ids=true, to_apply=%region_4.0 | all-reduce | flops 8192 | bytes 49152 | tf_op jit(solution)/shard_map/psum | solution.py:293
  1001.3 3.4 copy-done.5
  1004.7 2.2 copy-done.10
  1006.8 2.8 shard_map.95
  (36 shorter events, 0.4 us)
Async XLA Ops:
  7.2 116.8 %all-gather.9.cloned.1.call-start = ((), (), s32[]{:S(2)}) async-start(), calls=%async_computation.6 | async-start | bytes 20971520 | tf_op jit(solution)/shard_map/all_gather | solution.py:265
  8.0 3.4 copy-start
  15.8 2.0 copy-start.7
  17.9 211.3 %all-gather.13.cloned.1.call-start = ((), (), s32[]{:S(2)}) async-start(), calls=%async_computation.11 | async-start | bytes 20971520 | tf_op jit(solution)/shard_map/all_gather | solution.py:265
  23.9 367.8 %all-gather.7.cloned.1.call-start = ((), (), s32[]{:S(2)}) async-start(), calls=%async_computation.4 | async-start | bytes 20971520 | tf_op jit(solution)/shard_map/all_gather | solution.py:265
  24.0 4.7 copy-start.1
  33.2 2.0 copy-start.6
  35.2 449.8 %all-gather.11.cloned.1.call-start = ((), (), s32[]{:S(2)}) async-start(), calls=%async_computation.10 | async-start | bytes 20971520 | tf_op jit(solution)/shard_map/all_gather | solution.py:265
  35.8 908.6 %reduce-scatter.11.cloned.1.call-start = ((), (), s32[]{:S(2)}) async-start(), calls=%async_computation.9 | async-start | bytes 20971520 | tf_op jit(solution)/shard_map/reduce_scatter | solution.py:268
  216.7 1.9 copy-start.12
  275.8 2.3 copy-start.15
  391.7 571.1 %reduce-scatter.9.cloned.1.call-start = ((), (), s32[]{:S(2)}) async-start(), calls=%async_computation.8 | async-start | bytes 20971520 | tf_op jit(solution)/shard_map/reduce_scatter | solution.py:268
  483.1 1.9 copy-start.13
  530.0 2.2 copy-start.14
  635.4 345.7 %reduce-scatter.7.cloned.1.call-start = ((), (), s32[]{:S(2)}) async-start(), calls=%async_computation.7 | async-start | bytes 20971520 | tf_op jit(solution)/shard_map/reduce_scatter | solution.py:268
  678.4 322.8 %reduce-scatter.5.cloned.1.call-start = ((), (), s32[]{:S(2)}) async-start(), calls=%async_computation.5 | async-start | bytes 20971520 | tf_op jit(solution)/shard_map/reduce_scatter | solution.py:268
  944.4 3.4 copy-start.2
  947.8 2.4 copy-start.8
  962.7 3.6 copy-start.3
  966.3 2.2 copy-start.11
  981.1 3.5 copy-start.4
  984.6 2.2 copy-start.9
  1001.3 3.4 copy-start.5
  1004.7 2.2 copy-start.10
Sparse Core Ops, SparseCore 0:
  18.0 105.9 all-gather.8
  126.0 103.1 all-gather.12
  231.3 103.1 all-gather.6
  336.4 103.1 all-gather.10
  441.9 119.4 reduce-scatter.10
  635.5 119.2 reduce-scatter.8
  757.3 119.4 reduce-scatter.6
  879.4 119.8 reduce-scatter.4

commit v2 on v1

v2 whole, which is shorter than its diff:
```python
import functools
import jax
import jax.numpy as jnp
from jax import lax
from jax.experimental import pallas as pl
from jax.experimental.pallas import tpu as pltpu
from jax.sharding import PartitionSpec as P

CLIP_QKV = 8.0
ROPE_THETA = 500000.0
LN_EPS = 1e-5
LOG2E = 1.4426950408889634
QBLK = 256
NT = (((1,), (1,)), ((), ()))
NN = (((1,), (0,)), ((), ()))
TN = (((0,), (0,)), ((), ()))


def dot32(a, b, dims):
    return lax.dot_general(a, b, dims, preferred_element_type=jnp.float32)


def ln_stats(x):
    row_mean = jnp.mean(x, axis=-1, keepdims=True)
    centered = x - row_mean
    variance = jnp.mean(centered * centered, axis=-1, keepdims=True)
    rstd = lax.rsqrt(variance + LN_EPS)
    return centered * rstd, rstd


def ln_fwd_kernel(x_ref, gain_ref, h_ref):
    normed, _ = ln_stats(x_ref[0].astype(jnp.float32))
    h_ref[...] = (normed * gain_ref[...].astype(jnp.float32)).astype(jnp.bfloat16)


def ln_bwd_kernel(dh_ref, x_ref, dy_ref, gain_ref, *refs):
    dx_ref, dgain_ref = refs[-2:]
    normed, rstd = ln_stats(x_ref[0].astype(jnp.float32))
    d_h = dh_ref[...].astype(jnp.float32)
    d_gain = jnp.sum(d_h * normed, axis=0, keepdims=True)
    d_normed = d_h * gain_ref[...].astype(jnp.float32)
    shift = jnp.mean(d_normed, axis=-1, keepdims=True)
    slope = jnp.mean(d_normed * normed, axis=-1, keepdims=True)
    d_x = rstd * (d_normed - shift - normed * slope)
    dx_ref[0] = (dy_ref[0].astype(jnp.float32) + d_x).astype(jnp.bfloat16)

    @pl.when(pl.program_id(0) == 0)
    def _():
        dgain_ref[...] = d_gain

    @pl.when(pl.program_id(0) > 0)
    def _():
        dgain_ref[...] += d_gain


def residual_kernel(o_ref, x_ref, *refs):
    y_ref = refs[-1]
    y_ref[0] = (x_ref[0].astype(jnp.float32) + o_ref[...].astype(jnp.float32)).astype(jnp.bfloat16)


def rope_tables(seq_len, head_dim):
    inv_freq = 1.0 / (ROPE_THETA ** (jnp.arange(0, head_dim, 2, dtype=jnp.float32) / head_dim))
    angles = jnp.arange(seq_len, dtype=jnp.float32)[:, None] * inv_freq[None, :]
    cos_t, sin_t = jnp.cos(angles), jnp.sin(angles)
    return jnp.concatenate([cos_t, cos_t], axis=-1), jnp.concatenate([-sin_t, sin_t], axis=-1)


def clip(v):
    return jnp.minimum(jnp.maximum(v, -CLIP_QKV), CLIP_QKV)


def rope(v_f32, cos_t, sin_t):
    return v_f32 * cos_t + pltpu.roll(v_f32, v_f32.shape[-1] // 2, 1) * sin_t


def unrope(v_f32, cos_t, sin_t):
    return v_f32 * cos_t - pltpu.roll(v_f32, v_f32.shape[-1] // 2, 1) * sin_t


def masked_tail(s, fill):
    top, tail = s[:-QBLK], s[-QBLK:]
    rows = lax.broadcasted_iota(jnp.int32, tail.shape, 0)
    cols = lax.broadcasted_iota(jnp.int32, tail.shape, 1)
    tail = jnp.where(rows <= cols, tail, fill)
    return tail if s.shape[0] == QBLK else jnp.concatenate([top, tail], axis=0)


def half_rows(chip_ref, seq):
    half = seq // 2
    own = pl.multiple_of(chip_ref[0] * half, half)
    return half, pl.ds(own, half), pl.ds(half - own, half)


def join(chip_ref, own_ref, oth_ref, dst):
    _, own, oth = half_rows(chip_ref, dst.shape[0])
    dst[own, :] = own_ref[...].reshape(own_ref.shape[-2:])
    dst[oth, :] = oth_ref[...].reshape(oth_ref.shape[-2:])


def split(chip_ref, src, dst_ref):
    half, own, oth = half_rows(chip_ref, src.shape[-2])
    at = (0,) * (len(src.shape) - 2)
    dst_ref[at + (slice(0, half),)] = src[at + (own,)]
    dst_ref[at + (slice(half, 2 * half),)] = src[at + (oth,)]


def attn_fwd_kernel(groups, dim, chip_ref, own_ref, oth_ref, cos_ref, sin_ref, out_ref, perm_ref, lse_ref,
                    qkv_scr, k_scr, vt_scr):
    head = pl.program_id(1)
    seq = qkv_scr.shape[0]

    @pl.when(head == 0)
    def _():
        join(chip_ref, own_ref, oth_ref, qkv_scr)
        k_in = clip(qkv_scr[:, groups * dim:(groups + 1) * dim].astype(jnp.float32))
        k_scr[...] = rope(k_in, cos_ref[...], sin_ref[...]).astype(jnp.bfloat16)
        v_in = clip(qkv_scr[:, (groups + 1) * dim:(groups + 2) * dim].astype(jnp.float32))
        vt_scr[...] = v_in.T.astype(jnp.bfloat16)

    col = pl.ds(pl.multiple_of(head * dim, dim), dim)
    scale = LOG2E * dim ** -0.5

    def scores(i):
        rows = slice(i * QBLK, (i + 1) * QBLK)
        q_in = clip(qkv_scr[rows, col].astype(jnp.float32))
        q_rot = rope(q_in, cos_ref[rows, :], sin_ref[rows, :]).astype(jnp.bfloat16)
        return dot32(k_scr[:(i + 1) * QBLK, :], q_rot, NT)

    for i in range(seq // QBLK):
        rows = slice(i * QBLK, (i + 1) * QBLK)
        s = masked_tail(scores(i) * scale, -1e30)
        top = jnp.max(s, axis=0, keepdims=True)
        e = jnp.exp2(s - top)
        total = jnp.sum(e, axis=0, keepdims=True)
        prob = (e * (1.0 / total)).astype(jnp.bfloat16)
        o_t = dot32(vt_scr[:, :(i + 1) * QBLK], prob, NN)
        out_ref[rows, col] = o_t.T.astype(jnp.bfloat16)
        lse_ref[0, pl.ds(head, 1), rows] = top + jnp.log2(total)

    @pl.when(head == groups - 1)
    def _():
        split(chip_ref, out_ref, perm_ref)


def attn_bwd_kernel(groups, dim, chip_ref, own_ref, oth_ref, do_own_ref, do_oth_ref, lse_ref, cos_ref, sin_ref,
                    dqkv_ref, perm_ref, qkv_scr, do_scr, k_scr, kt_scr, v_scr, dk_scr, dv_scr):
    head = pl.program_id(1)
    seq = qkv_scr.shape[0]
    kcol = slice(groups * dim, (groups + 1) * dim)
    vcol = slice((groups + 1) * dim, (groups + 2) * dim)

    @pl.when(head == 0)
    def _():
        join(chip_ref, own_ref, oth_ref, qkv_scr)
        join(chip_ref, do_own_ref, do_oth_ref, do_scr)
        k_in = clip(qkv_scr[:, kcol].astype(jnp.float32))
        k_rot = rope(k_in, cos_ref[...], sin_ref[...])
        k_scr[...] = k_rot.astype(jnp.bfloat16)
        kt_scr[...] = k_rot.T.astype(jnp.bfloat16)
        v_scr[...] = clip(qkv_scr[:, vcol].astype(jnp.float32)).astype(jnp.bfloat16)
        dk_scr[...] = jnp.zeros_like(dk_scr)
        dv_scr[...] = jnp.zeros_like(dv_scr)

    col = pl.ds(pl.multiple_of(head * dim, dim), dim)
    scale = dim ** -0.5
    for i in range(seq // QBLK):
        rows = slice(i * QBLK, (i + 1) * QBLK)
        kend = (i + 1) * QBLK
        q_raw = qkv_scr[rows, col].astype(jnp.float32)
        q_rot = rope(clip(q_raw), cos_ref[rows, :], sin_ref[rows, :]).astype(jnp.bfloat16)
        d_o = do_scr[rows, col]
        s = dot32(k_scr[:kend, :], q_rot, NT) * (LOG2E * scale) - lse_ref[0, pl.ds(head, 1), rows]
        p = jnp.exp2(masked_tail(s, -1e30))
        dv_scr[:kend, :] += dot32(p.astype(jnp.bfloat16), d_o, NN)
        dp = dot32(v_scr[:kend, :], d_o, NT).astype(jnp.bfloat16).astype(jnp.float32)
        t = p * dp
        delta = jnp.sum(t, axis=0, keepdims=True)
        ds = (t - p * delta).astype(jnp.bfloat16)
        dk_scr[:kend, :] += dot32(ds, q_rot, NN)
        dq = (dot32(kt_scr[:, :kend], ds, NN) * scale).T.astype(jnp.bfloat16).astype(jnp.float32)
        dq = unrope(dq, cos_ref[rows, :], sin_ref[rows, :])
        dqkv_ref[0, rows, col] = jnp.where(jnp.abs(q_raw) < CLIP_QKV, dq, 0.0).astype(jnp.bfloat16)

    @pl.when(head == groups - 1)
    def _():
        k_raw = qkv_scr[:, kcol].astype(jnp.float32)
        v_raw = qkv_scr[:, vcol].astype(jnp.float32)
        dk = (dk_scr[...] * scale).astype(jnp.bfloat16).astype(jnp.float32)
        dk = unrope(dk, cos_ref[...], sin_ref[...])
        dqkv_ref[0, :, kcol] = jnp.where(jnp.abs(k_raw) < CLIP_QKV, dk, 0.0).astype(jnp.bfloat16)
        dqkv_ref[0, :, vcol] = jnp.where(jnp.abs(v_raw) < CLIP_QKV, dv_scr[...], 0.0).astype(jnp.bfloat16)
        split(chip_ref, dqkv_ref, perm_ref)


VMEM_MAX = 63 * 2 ** 20


def attn_params(kv_loc, groups, seq, dim, dots):
    return dict(
        compiler_params=pltpu.CompilerParams(dimension_semantics=("arbitrary", "arbitrary"),
                                             vmem_limit_bytes=VMEM_MAX),
        cost_estimate=pl.CostEstimate(flops=dots * 2 * kv_loc * groups * seq * seq * dim,
                                      bytes_accessed=2 * kv_loc * seq * dim * (2 * groups + 2) * 2,
                                      transcendentals=kv_loc * groups * seq * seq // 2))


def attn_fwd(chip, own, oth, cos_t, sin_t, dim):
    kv_loc, half, width = own.shape
    seq = 2 * half
    groups = width // dim - 2
    table = pl.BlockSpec((seq, dim), lambda n, h: (0, 0))
    piece = pl.BlockSpec((1, half, width), lambda n, h: (n, 0, 0))
    heads = pl.BlockSpec((seq, groups * dim), lambda n, h: (0, n))
    heads_shape = jax.ShapeDtypeStruct((seq, kv_loc * groups * dim), jnp.bfloat16)
    return pl.pallas_call(
        functools.partial(attn_fwd_kernel, groups, dim),
        grid=(kv_loc, groups),
        in_specs=[pl.BlockSpec(memory_space=pltpu.SMEM), piece, piece, table, table],
        out_specs=[heads, heads, pl.BlockSpec((1, groups, seq), lambda n, h: (n, 0, 0))],
        out_shape=[heads_shape, heads_shape, jax.ShapeDtypeStruct((kv_loc, groups, seq), jnp.float32)],
        scratch_shapes=[pltpu.VMEM((seq, width), jnp.bfloat16), pltpu.VMEM((seq, dim), jnp.bfloat16),
                        pltpu.VMEM((dim, seq), jnp.bfloat16)],
        name="attn_fwd",
        **attn_params(kv_loc, groups, seq, dim, 4),
    )(chip, own, oth, cos_t, sin_t)


def attn_bwd(chip, own, oth, do_own, do_oth, lse, cos_t, sin_t, dim):
    kv_loc, half, width = own.shape
    seq = 2 * half
    groups = width // dim - 2
    table = pl.BlockSpec((seq, dim), lambda n, h: (0, 0))
    piece = pl.BlockSpec((1, half, width), lambda n, h: (n, 0, 0))
    d_piece = pl.BlockSpec((half, groups * dim), lambda n, h: (0, n))
    wide = pl.BlockSpec((1, seq, width), lambda n, h: (n, 0, 0))
    wide_shape = jax.ShapeDtypeStruct((kv_loc, seq, width), jnp.bfloat16)
    return pl.pallas_call(
        functools.partial(attn_bwd_kernel, groups, dim),
        grid=(kv_loc, groups),
        in_specs=[pl.BlockSpec(memory_space=pltpu.SMEM), piece, piece, d_piece, d_piece,
                  pl.BlockSpec((1, groups, seq), lambda n, h: (n, 0, 0)), table, table],
        out_specs=[wide, wide],
        out_shape=[wide_shape, wide_shape],
        scratch_shapes=[pltpu.VMEM((seq, width), jnp.bfloat16), pltpu.VMEM((seq, groups * dim), jnp.bfloat16),
                        pltpu.VMEM((seq, dim), jnp.bfloat16), pltpu.VMEM((dim, seq), jnp.bfloat16),
                        pltpu.VMEM((seq, dim), jnp.bfloat16), pltpu.VMEM((seq, dim), jnp.float32),
                        pltpu.VMEM((seq, dim), jnp.float32)],
        name="attn_bwd",
        **attn_params(kv_loc, groups, seq, dim, 8),
    )(chip, own, oth, do_own, do_oth, lse, cos_t, sin_t)


def wqkv_grad_kernel(pieces, *refs):
    h_refs, d_refs, out_ref = refs[:pieces], refs[pieces:-1], refs[-1]
    half = h_refs[0].shape[0]
    for n in range(out_ref.shape[1]):
        total = 0.0
        for j in range(pieces):
            at = half * (j % 2)
            total += dot32(h_refs[j][...], d_refs[j // 2][n, at:at + half, :], TN)
        out_ref[:, n, :] = total.astype(jnp.bfloat16)


def wqkv_grad_call(h_pieces, d_qkv):
    half, rows = h_pieces[0].shape
    kv_loc, seq, width = d_qkv[0].shape
    block = 256
    return pl.pallas_call(
        functools.partial(wqkv_grad_kernel, len(h_pieces)), grid=(rows // block,),
        in_specs=[pl.BlockSpec((half, block), lambda r: (0, r))] * len(h_pieces)
        + [pl.BlockSpec((kv_loc, seq, width), lambda r: (0, 0, 0))] * len(d_qkv),
        out_specs=pl.BlockSpec((block, kv_loc, width), lambda r: (r, 0, 0)),
        out_shape=jax.ShapeDtypeStruct((rows, kv_loc, width), jnp.bfloat16),
        compiler_params=pltpu.CompilerParams(dimension_semantics=("arbitrary",), vmem_limit_bytes=VMEM_MAX),
        cost_estimate=pl.CostEstimate(flops=2 * half * len(h_pieces) * rows * kv_loc * width,
                                      bytes_accessed=4 * rows * kv_loc * width, transcendentals=0),
        name="wqkv_grad",
    )(*h_pieces, *d_qkv)


def row_call(body, rows, b, flat_in, full_in, extra_in, prev, extra_out):
    tokens, width = full_in[0].shape[1:]
    flat = pl.BlockSpec((rows, width), lambda r: (r, 0))
    full = pl.BlockSpec((1, rows, width), lambda r: (b, r, 0))
    wide = pl.BlockSpec((1, width), lambda r: (0, 0))
    args = [*flat_in, *full_in, *extra_in] + ([] if prev is None else [prev])
    specs = [flat] * len(flat_in) + [full] * len(full_in) + [wide] * len(extra_in)
    if prev is not None:
        specs.append(pl.BlockSpec(memory_space=pl.ANY))
    out_spec = flat if prev is None and not flat_in else full
    out_shape = (tokens, width) if prev is None and not flat_in else full_in[0].shape
    out_shape = [jax.ShapeDtypeStruct(out_shape, jnp.bfloat16)]
    out_shape += [jax.ShapeDtypeStruct((1, width), jnp.float32)] * extra_out
    return pl.pallas_call(
        body, grid=(tokens // rows,), in_specs=specs, out_specs=[out_spec] + [wide] * extra_out, out_shape=out_shape,
        input_output_aliases={} if prev is None else {len(args) - 1: 0},
        compiler_params=pltpu.CompilerParams(dimension_semantics=("arbitrary",), vmem_limit_bytes=VMEM_MAX),
        cost_estimate=pl.CostEstimate(flops=40 * tokens * width, bytes_accessed=2 * len(args) * tokens * width,
                                      transcendentals=0),
    )(*args)


def ein(spec, a, b):
    return jnp.einsum(spec, a, b, preferred_element_type=jnp.float32).astype(jnp.bfloat16)


def solution(mesh):
    def device_step(x_seq, ln_gain, w_qkv, w_out, y_grad):
        batch = x_seq.shape[0]
        kv_loc = w_qkv.shape[1]
        dim = (w_qkv.shape[2] - w_out.shape[0] // kv_loc) // 2
        gain = ln_gain.reshape(1, -1)
        cos_t, sin_t = rope_tables(x_seq.shape[1] * lax.axis_size('tp'), dim)
        chip = (lax.axis_index('tp') // 2).astype(jnp.int32).reshape(1)

        def across(v):
            return lax.ppermute(v, 'tp', [(d, (d + 2) % 4) for d in range(4)])

        def pair(v):
            return lax.all_gather(v, 'tp', axis=0, tiled=True, axis_index_groups=[[0, 1], [2, 3]])

        def scatter(v):
            return lax.psum_scatter(v, 'tp', scatter_dimension=0, tiled=True)

        seqs = range(batch)
        h_loc = [row_call(ln_fwd_kernel, 32, b, [], [x_seq], [gain], None, 0)[0] for b in seqs]
        g_loc = [y_grad[b] for b in seqs]
        h_far = [across(h_loc[b]) for b in seqs]
        g_far = [across(g_loc[b]) for b in seqs]
        h_own = [pair(h_loc[b]) for b in seqs]
        g_own = [pair(g_loc[b]) for b in seqs]
        h_oth = [pair(h_far[b]) for b in seqs]
        g_oth = [pair(g_far[b]) for b in seqs]
        qkv_own = [ein('sd,dnc->nsc', h_own[b], w_qkv) for b in seqs]
        d_own = [ein('sd,kd->sk', g_own[b], w_out) for b in seqs]
        qkv_oth, attn_perm, lse, outs, d_perm, dhs = [], [], [], [], [], []
        for b in seqs:
            qkv_oth.append(ein('sd,dnc->nsc', h_oth[b], w_qkv))
            a_seq, a_perm, lse_b = attn_fwd(chip, qkv_own[b], qkv_oth[b], cos_t, sin_t, dim)
            attn_perm.append(a_perm)
            lse.append(lse_b)
            outs.append(scatter(ein('sk,kd->sd', a_seq, w_out)))
        for b in seqs:
            d_oth = ein('sd,kd->sk', g_oth[b], w_out)
            d_seq, d_perm_b = attn_bwd(chip, qkv_own[b], qkv_oth[b], d_own[b], d_oth, lse[b], cos_t, sin_t, dim)
            d_perm.append(d_perm_b)
            dhs.append(scatter(ein('nsc,dnc->sd', d_seq, w_qkv)))
        g_all = jnp.concatenate([v for b in seqs for v in (g_own[b], g_oth[b])], 0)
        wout_grad = ein('sk,sd->kd', jnp.concatenate(attn_perm, 0), g_all)
        wqkv_grad = wqkv_grad_call([v for b in seqs for v in (h_own[b], h_oth[b])], d_perm)
        y_out, x_grad, gain_part = None, None, 0.0
        for b in seqs:
            (y_out,) = row_call(residual_kernel, 64, b, [outs[b]], [x_seq], [], y_out, 0)
        for b in seqs:
            x_grad, gain_b = row_call(ln_bwd_kernel, 32, b, [dhs[b]], [x_seq, y_grad], [gain], x_grad, 1)
            gain_part = gain_part + gain_b[0]
        gain_grad = lax.psum(gain_part, 'tp').astype(jnp.bfloat16)
        return y_out, x_grad, gain_grad, wqkv_grad, wout_grad

    specs_in = (P('dp', 'tp', None), P(None), P(None, 'tp', None), P('tp', None), P('dp', 'tp', None))
    specs_out = (P('dp', 'tp', None), P('dp', 'tp', None), P('dp'), P('dp', 'tp', None), P(('dp', 'tp'), None))
    return jax.shard_map(device_step, mesh=mesh, in_specs=specs_in, out_specs=specs_out, check_vma=False)
```

time: 1030 us -> 1300 us (1.26)
  waiting for transfers between devices: 97 us -> 400 us
  Pallas kernels: 264 us -> 357 us
  matrix products: 577 us -> 488 us
  local copies, waits for them, and re-layouts: 49.9 us -> 10.8 us
    ppermute x0 -> x4, waiting for transfers between devices: none -> 355 us  [across(): return lax.ppermute(v, 'tp', [(d, (d + 2) % 4) for d in range(4)])]
    all_gather x4 -> x8, waiting for transfers between devices: 96.3 us -> 0.06 us  [pair(): lax.all_gather(v, 'tp', axis=0, tiled=True, axis_index_groups=[[0, 1], [2...]
    dot_general x10 -> x13, matrix products: 577 us -> 488 us  [ein(): jnp.einsum(spec, a, b, preferred_element_type=jnp.float32)]
    pallas_call x1, Pallas kernels: 46.4 us -> 110 us  [wqkv_grad_call(): pl.pallas_call(functools.partial(wqkv_grad_kernel, len(h_pieces)), grid=(...]
    reduce_scatter x4, waiting for transfers between devices: 0.03 us -> 43.7 us  [scatter(): return lax.psum_scatter(v, 'tp', scatter_dimension=0, tiled=True)]
    unnamed x32 -> x2, local copies, waits for them, and re-layouts: 43.2 us -> 0.01 us
    pallas_call x6, Pallas kernels: 39.6 us -> 57 us  [row_call(): pl.pallas_call(body, grid=(tokens // rows,), in_specs=specs, out_specs=[o...]
  transfers between devices with their start and end apart: 8 -> 16, of which waited for: 2 -> 5; matrix products, arithmetic and copies ran while one was open for 58% -> 39% of each run, Pallas kernels for 25% -> 26%
where the time goes in v2:
time: 1300 us
  matrix products  488 us (38%)
  waiting for transfers between devices  400 us (31%)
  Pallas kernels  357 us (27%)
  between operations  14.5 us (1%)
    dot_general x13, matrix products, ein(): jnp.einsum(spec, a, b, preferred_element_type=jnp.float32)  488 us
    ppermute x4, waiting for transfers between devices, across(): return lax.ppermute(v, 'tp', [(d, (d + 2) % 4) for d in range(4)])  355 us
    pallas_call x1, Pallas kernels, wqkv_grad_call(): pl.pallas_call(functools.partial(wqkv_grad_kernel, len(h_pieces)), grid=(...  110 us
    pallas_call x2, Pallas kernels, attn_bwd(): pl.pallas_call(functools.partial(attn_bwd_kernel, groups, dim), grid=(kv_...  109 us
    pallas_call x2, Pallas kernels, attn_fwd(): pl.pallas_call(functools.partial(attn_fwd_kernel, groups, dim), grid=(kv_...  82 us
    pallas_call x6, Pallas kernels, row_call(): pl.pallas_call(body, grid=(tokens // rows,), in_specs=specs, out_specs=[o...  57 us
    reduce_scatter x4, waiting for transfers between devices, scatter(): return lax.psum_scatter(v, 'tp', scatter_dimension=0, tiled=True)  43.7 us
  transfers between devices with their start and end apart: 16, of which 5 were waited for; matrix products, arithmetic and copies ran while one was open for 39% of the time, Pallas kernels for 26%

profile of v2, /device:TPU:0, one launch (start us, length us, event | category | flops | bytes accessed | tf_op | source)
XLA Modules:
  0.0 1296.3 jit_solution(6225905574841146525)
XLA Ops:
  7.2 1.3 reshape.24.gain_ref
  8.5 8.5 shard_map.93
  17.0 0.0 all-gather.25.cloned.1.call-start
  17.1 9.5 slice_bitcast_fusion
  26.6 0.0 all-gather.17.cloned.1.call-start
  26.6 4.3 collective-permute-start.1
  30.9 90.6 %collective-permute-done.1 = bf16[256,8192]{1,0:T(8,128)(2,1)} collective-permute-done((bf16[256,8192]{1,0:T(8,128)(2,1)}, bf16[256,8192]{1,0:T(8,128)(2,1)}, u32[]{:S(2)}, u32[]{:S(2)}) %collective-permute-start.1) | collective-permute-done | bytes 4194336 | tf_op jit(solution)/shard_map/ppermute | solution.py:317
  121.6 1.8 collective-permute-start.3
  123.3 90.0 %collective-permute-done.3 = bf16[256,8192]{1,0:T(8,128)(2,1)} collective-permute-done((bf16[256,8192]{1,0:T(8,128)(2,1)}, bf16[256,8192]{1,0:T(8,128)(2,1)}, u32[]{:S(2)}, u32[]{:S(2)}) %collective-permute-start.3) | collective-permute-done | bytes 4194336 | tf_op jit(solution)/shard_map/ppermute | solution.py:317
  213.4 0.5 all-gather.23.cloned.1.call-update
  213.9 0.0 all-gather.11.cloned.1.call-start
  214.0 8.7 shard_map.92
  222.7 0.0 all-gather.13.cloned.1.call-start
  222.8 1.5 collective-permute-start
  224.2 89.3 %collective-permute-done = bf16[256,8192]{1,0:T(8,128)(2,1)} collective-permute-done((bf16[256,8192]{1,0:T(8,128)(2,1)}, bf16[256,8192]{1,0:T(8,128)(2,1)}, u32[]{:S(2)}, u32[]{:S(2)}) %collective-permute-start) | collective-permute-done | bytes 4194336 | tf_op jit(solution)/shard_map/ppermute | solution.py:317
  313.6 1.4 collective-permute-start.2
  315.0 2.0 fusion.70
  317.0 1.3 pad_maximum_fusion
  318.3 85.2 %collective-permute-done.2 = bf16[256,8192]{1,0:T(8,128)(2,1)} collective-permute-done((bf16[256,8192]{1,0:T(8,128)(2,1)}, bf16[256,8192]{1,0:T(8,128)(2,1)}, u32[]{:S(2)}, u32[]{:S(2)}) %collective-permute-start.2) | collective-permute-done | bytes 4194336 | tf_op jit(solution)/shard_map/ppermute | solution.py:317
  403.5 0.2 reduce-scatter.11.cloned.1.call-start
  403.8 30.6 %fusion.53.own_ref = bf16[2,512,1280]{2,1,0:T(8,128)(2,1)} fusion(bf16[8192,2,1280]{2,1,0:T(2,128)(2,1)} %param.7, bf16[512,8192]{1,0:T(8,128)(2,1)} %all-gather.15.cloned.1.call-done.refs_0_), kind=kOutput, calls=%fused_computation.35 | convolution fusion | flops 21476147200 | bytes 52953088 | tf_op jit(solution)/shard_map/sd,dnc->nsc/dot_general | solution.py:304
  434.4 24.7 %convolution_convert_fusion.3.do_own_ref = bf16[512,2048]{1,0:T(8,128)(2,1)} fusion(bf16[2048,8192]{1,0:T(8,128)(2,1)} %param.8, bf16[1,512,8192]{2,1,0:T(8,128)(2,1)} %all-gather.25.cloned.1.call-done), kind=kOutput, calls=%fused_computation.39 | convolution fusion | flops 17180917760 | bytes 44040192 | tf_op jit(solution)/shard_map/sd,kd->sk/dot_general | solution.py:304
  459.1 29.3 %fusion.48.oth_ref = bf16[2,512,1280]{2,1,0:T(8,128)(2,1)} fusion(bf16[8192,2,1280]{2,1,0:T(2,128)(2,1)} %param.7, bf16[512,8192]{1,0:T(8,128)(2,1)} %all-gather.17.cloned.1.call-done.refs_1_), kind=kOutput, calls=%fused_computation.34 | convolution fusion | flops 21476147200 | bytes 52953088 | tf_op jit(solution)/shard_map/sd,dnc->nsc/dot_general | solution.py:304
  488.4 41.1 %attn_fwd.3 = (bf16[1024,2048]{1,0:T(8,128)(2,1)}, bf16[1024,2048]{1,0:T(8,128)(2,1)}, f32[2,8,1024]{2,1,0:T(8,128)}) custom-call(s32[1]{0:T(128)} %bitcast.chip_ref, bf16[2,512,1280]{2,1,0:T(8,128)(2,1)} %fusion.53.own_ref, bf16[2,512,1280]{2,1,0:T(8,128)(2,1)} %fusion.48.oth_ref, f32[1024,128]{1,0:T(8,128)} %get-tuple-element.40.cos_ref, ...), custom_call_target="tpu_custom_call" | custom-call | flops 17179869184 | bytes 18874368 | tf_op jit(solution)/shard_map/attn_fwd/pallas_call | solution.py:215
  529.5 24.8 %convolution_convert_fusion.2.do_oth_ref = bf16[512,2048]{1,0:T(8,128)(2,1)} fusion(bf16[512,8192]{1,0:T(8,128)(2,1)} %all-gather.21.cloned.1.call-done, bf16[2048,8192]{1,0:T(8,128)(2,1)} %param.8), kind=kOutput, calls=%fused_computation.38 | convolution fusion | flops 17180917760 | bytes 44040192 | tf_op jit(solution)/shard_map/sd,kd->sk/dot_general | solution.py:304
  554.3 54.4 %attn_bwd.3 = (bf16[2,1024,1280]{2,1,0:T(8,128)(2,1)}, bf16[2,1024,1280]{2,1,0:T(8,128)(2,1)}) custom-call(s32[1]{0:T(128)} %bitcast.chip_ref, bf16[2,512,1280]{2,1,0:T(8,128)(2,1)} %fusion.53.own_ref, bf16[2,512,1280]{2,1,0:T(8,128)(2,1)} %fusion.48.oth_ref, bf16[512,2048]{1,0:T(8,128)(2,1)} %convolution_convert_fusion.3.do_own_ref, ...), custom_call_target="tpu_custom_call" | custom-call | flops 34359738368 | bytes 18874368 | tf_op jit(solution)/shard_map/attn_bwd/pallas_call | solution.py:237
  608.7 51.3 %bitcast_convert_fusion = bf16[1024,8192]{1,0:T(8,128)(2,1)} fusion(bf16[2,1024,1280]{2,1,0:T(8,128)(2,1)} %get-tuple-element.24, bf16[8192,2,1280]{2,1,0:T(2,128)(2,1)} %param.7), kind=kOutput, calls=%fused_computation.8 | convolution fusion | flops 42958061568 | bytes 63963136 | tf_op jit(solution)/shard_map/nsc,dnc->sd/dot_general | solution.py:304
  660.0 0.0 reduce-scatter.9.cloned.1.call-start
  660.1 27.8 %convolution_convert_fusion.5.do_own_ref = bf16[512,2048]{1,0:T(8,128)(2,1)} fusion(bf16[2048,8192]{1,0:T(8,128)(2,1)} %param.8, bf16[1,512,8192]{2,1,0:T(8,128)(2,1)} %all-gather.23.cloned.1.call-done), kind=kOutput, calls=%fused_computation.41 | convolution fusion | flops 17180917760 | bytes 44040192 | tf_op jit(solution)/shard_map/sd,kd->sk/dot_general | solution.py:304
  687.9 29.4 %fusion.63.own_ref = bf16[2,512,1280]{2,1,0:T(8,128)(2,1)} fusion(bf16[8192,2,1280]{2,1,0:T(2,128)(2,1)} %param.7, bf16[512,8192]{1,0:T(8,128)(2,1)} %all-gather.11.cloned.1.call-done.refs_2_), kind=kOutput, calls=%fused_computation.37 | convolution fusion | flops 21476147200 | bytes 52953088 | tf_op jit(solution)/shard_map/sd,dnc->nsc/dot_general | solution.py:304
  717.3 29.6 %fusion.58.oth_ref = bf16[2,512,1280]{2,1,0:T(8,128)(2,1)} fusion(bf16[8192,2,1280]{2,1,0:T(2,128)(2,1)} %param.7, bf16[512,8192]{1,0:T(8,128)(2,1)} %all-gather.13.cloned.1.call-done.refs_3_), kind=kOutput, calls=%fused_computation.36 | convolution fusion | flops 21476147200 | bytes 52953088 | tf_op jit(solution)/shard_map/sd,dnc->nsc/dot_general | solution.py:304
  746.9 40.8 %attn_fwd.2 = (bf16[1024,2048]{1,0:T(8,128)(2,1)}, bf16[1024,2048]{1,0:T(8,128)(2,1)}, f32[2,8,1024]{2,1,0:T(8,128)}) custom-call(s32[1]{0:T(128)} %bitcast.chip_ref, bf16[2,512,1280]{2,1,0:T(8,128)(2,1)} %fusion.63.own_ref, bf16[2,512,1280]{2,1,0:T(8,128)(2,1)} %fusion.58.oth_ref, f32[1024,128]{1,0:T(8,128)} %get-tuple-element.40.cos_ref, ...), custom_call_target="tpu_custom_call" | custom-call | flops 17179869184 | bytes 18874368 | tf_op jit(solution)/shard_map/attn_fwd/pallas_call | solution.py:215
  787.8 24.7 %convolution_convert_fusion.4.do_oth_ref = bf16[512,2048]{1,0:T(8,128)(2,1)} fusion(bf16[512,8192]{1,0:T(8,128)(2,1)} %all-gather.19.cloned.1.call-done, bf16[2048,8192]{1,0:T(8,128)(2,1)} %param.8), kind=kOutput, calls=%fused_computation.40 | convolution fusion | flops 17180917760 | bytes 44040192 | tf_op jit(solution)/shard_map/sd,kd->sk/dot_general | solution.py:304
  812.5 54.4 %attn_bwd.2 = (bf16[2,1024,1280]{2,1,0:T(8,128)(2,1)}, bf16[2,1024,1280]{2,1,0:T(8,128)(2,1)}) custom-call(s32[1]{0:T(128)} %bitcast.chip_ref, bf16[2,512,1280]{2,1,0:T(8,128)(2,1)} %fusion.63.own_ref, bf16[2,512,1280]{2,1,0:T(8,128)(2,1)} %fusion.58.oth_ref, bf16[512,2048]{1,0:T(8,128)(2,1)} %convolution_convert_fusion.5.do_own_ref, ...), custom_call_target="tpu_custom_call" | custom-call | flops 34359738368 | bytes 18874368 | tf_op jit(solution)/shard_map/attn_bwd/pallas_call | solution.py:237
  866.9 51.7 %bitcast_convert_fusion.1 = bf16[1024,8192]{1,0:T(8,128)(2,1)} fusion(bf16[2,1024,1280]{2,1,0:T(8,128)(2,1)} %get-tuple-element.22, bf16[8192,2,1280]{2,1,0:T(2,128)(2,1)} %param.7), kind=kOutput, calls=%fused_computation.9 | convolution fusion | flops 42958061568 | bytes 63963136 | tf_op jit(solution)/shard_map/nsc,dnc->sd/dot_general | solution.py:304
  918.6 0.0 reduce-scatter.7.cloned.1.call-start
  918.7 42.5 %convolution_convert_fusion = bf16[1024,8192]{1,0:T(8,128)(2,1)} fusion(bf16[1024,2048]{1,0:T(8,128)(2,1)} %get-tuple-element.20, bf16[2048,8192]{1,0:T(8,128)(2,1)} %param.8), kind=kOutput, calls=%fused_computation.21 | convolution fusion | flops 34368126976 | bytes 54525952 | tf_op jit(solution)/shard_map/sk,kd->sd/dot_general | solution.py:304
  961.2 0.0 reduce-scatter.5.cloned.1.call-start
  961.3 42.0 %convolution_convert_fusion.1 = bf16[1024,8192]{1,0:T(8,128)(2,1)} fusion(bf16[1024,2048]{1,0:T(8,128)(2,1)} %get-tuple-element.19, bf16[2048,8192]{1,0:T(8,128)(2,1)} %param.8), kind=kOutput, calls=%fused_computation.22 | convolution fusion | flops 34368126976 | bytes 54525952 | tf_op jit(solution)/shard_map/sk,kd->sd/dot_general | solution.py:304
  1003.3 109.6 %wqkv_grad.1 = bf16[8192,2,1280]{2,1,0:T(2,128)(2,1)} custom-call(bf16[512,8192]{1,0:T(8,128)(2,1)} %all-gather.15.cloned.1.call-done.refs_0_, bf16[512,8192]{1,0:T(8,128)(2,1)} %all-gather.17.cloned.1.call-done.refs_1_, bf16[512,8192]{1,0:T(8,128)(2,1)} %all-gather.11.cloned.1.call-done.refs_2_, bf16[512,8192]{1,0:T(8,128)(2,1)} %all-gather.13.cloned.1.call-done.refs_3_, ...), custom_call_target="tpu_custom_call" | custom-call | flops 85899345920 | bytes 83886080 | tf_op jit(solution)/shard_map/wqkv_grad/pallas_call | solution.py:268
  1112.9 79.4 %fusion.8 = bf16[2048,8192]{1,0:T(8,128)(2,1)} fusion(bf16[512,8192]{1,0:T(8,128)(2,1)} %all-gather.19.cloned.1.call-done, bf16[512,8192]{1,0:T(8,128)(2,1)} %bitcast.66, bf16[512,8192]{1,0:T(8,128)(2,1)} %all-gather.21.cloned.1.call-done, bf16[512,8192]{1,0:T(8,128)(2,1)} %bitcast.65, bf16[1024,2048]{1,0:T(8,128)(2,1)} %get-tuple-element.32, ...), kind=kOutput, calls=%fused_computation.10 | convolution fusion | flops 68887248896 | bytes 75497472 | tf_op jit(solution)/shard_map/sk,sd->kd/dot_general | solution.py:304
  1192.3 13.9 %shard_map.96 = (bf16[2,256,8192]{2,1,0:T(8,128)(2,1)}, f32[1,8192]{1,0:T(1,128)}) custom-call(bf16[256,8192]{1,0:T(8,128)(2,1)} %reduce-scatter.11.cloned.1.call-done.dh_ref, bf16[2,256,8192]{2,1,0:T(8,128)(2,1)} %x_ref.11, bf16[2,256,8192]{2,1,0:T(8,128)(2,1)} %dy_ref.3, bf16[1,8192]{1,0:T(2,128)(2,1)} %reshape.24.gain_ref), custom_call_target="tpu_custom_call" | custom-call | flops 83886080 | bytes 16777216 | tf_op jit(solution)/shard_map/pallas_call | solution.py:294
  1206.2 13.8 %shard_map.97 = (bf16[2,256,8192]{2,1,0:T(8,128)(2,1)}, f32[1,8192]{1,0:T(1,128)}) custom-call(bf16[256,8192]{1,0:T(8,128)(2,1)} %reduce-scatter.9.cloned.1.call-done.dh_ref, bf16[2,256,8192]{2,1,0:T(8,128)(2,1)} %x_ref.11, bf16[2,256,8192]{2,1,0:T(8,128)(2,1)} %dy_ref.3, bf16[1,8192]{1,0:T(2,128)(2,1)} %reshape.24.gain_ref, ...), custom_call_target="tpu_custom_call", output_to_operand_aliasing={{0}: (4, {})} | custom-call | flops 83886080 | bytes 20971520 | tf_op jit(solution)/shard_map/pallas_call | solution.py:294
  1220.0 0.8 add.17
  1220.8 6.1 shard_map.94.refs_0_
  1227.0 12.7 psum.7
  1239.6 43.6 %reduce-scatter.5.cloned.1.call-done.o_ref = bf16[256,8192]{1,0:T(8,128)(2,1)} async-done(((bf16[1024,8192]{1,0:T(8,128)(2,1)}), bf16[256,8192]{1,0:T(8,128)(2,1)}) %reduce-scatter.5.cloned.1.call-update) | async-done | bytes 4194320 | tf_op jit(solution)/shard_map/reduce_scatter | solution.py:323
  1283.3 6.0 shard_map.95
  (29 shorter events, 0.4 us)
Async XLA Ops:
  7.2 396.6 %all-gather.15.cloned.1.call-start = ((), (), s32[]{:S(2)}) async-start(), calls=%async_computation.7 | async-start | bytes 12582912 | tf_op jit(solution)/shard_map/all_gather | solution.py:320
  17.0 417.3 %all-gather.25.cloned.1.call-start = ((), (), s32[]{:S(2)}) async-start(), calls=%async_computation.15 | async-start | bytes 12582912 | tf_op jit(solution)/shard_map/all_gather | solution.py:320
  26.6 432.5 %all-gather.17.cloned.1.call-start = ((), (), s32[]{:S(2)}) async-start(), calls=%async_computation.8 | async-start | bytes 12582912 | tf_op jit(solution)/shard_map/all_gather | solution.py:320
  26.6 94.9 %collective-permute-start.1 = (bf16[256,8192]{1,0:T(8,128)(2,1)}, bf16[256,8192]{1,0:T(8,128)(2,1)}, u32[]{:S(2)}, u32[]{:S(2)}) collective-permute-start(bf16[256,8192]{1,0:T(8,128)(2,1)} %shard_map.93), channel_id=1, source_target_pairs={{0,2},{1,3},{2,0},{3,1},{4,6},{5,7},{6,4},{7,5}} | collective-permute-start | bytes 12582920 | tf_op jit(solution)/shard_map/ppermute | solution.py:317
  121.5 408.0 %all-gather.21.cloned.1.call-start = ((), (), s32[]{:S(2)}) async-start(), calls=%async_computation.12 | async-start | bytes 12582912 | tf_op jit(solution)/shard_map/all_gather | solution.py:320
  121.6 91.7 %collective-permute-start.3 = (bf16[256,8192]{1,0:T(8,128)(2,1)}, bf16[256,8192]{1,0:T(8,128)(2,1)}, u32[]{:S(2)}, u32[]{:S(2)}) collective-permute-start(bf16[256,8192]{1,0:T(8,128)(2,1)} %get-tuple-element.33), channel_id=1, source_target_pairs={{0,2},{1,3},{2,0},{3,1},{4,6},{5,7},{6,4},{7,5}} | collective-permute-start | bytes 12582920 | tf_op jit(solution)/shard_map/ppermute | solution.py:317
  213.3 446.7 %all-gather.23.cloned.1.call-start = ((), (), s32[]{:S(2)}) async-start(), calls=%async_computation.14 | async-start | bytes 12582912 | tf_op jit(solution)/shard_map/all_gather | solution.py:320
  213.9 474.0 %all-gather.11.cloned.1.call-start = ((), (), s32[]{:S(2)}) async-start(), calls=%async_computation.4 | async-start | bytes 12582912 | tf_op jit(solution)/shard_map/all_gather | solution.py:320
  222.7 494.6 %all-gather.13.cloned.1.call-start = ((), (), s32[]{:S(2)}) async-start(), calls=%async_computation.5 | async-start | bytes 12582912 | tf_op jit(solution)/shard_map/all_gather | solution.py:320
  222.8 90.8 %collective-permute-start = (bf16[256,8192]{1,0:T(8,128)(2,1)}, bf16[256,8192]{1,0:T(8,128)(2,1)}, u32[]{:S(2)}, u32[]{:S(2)}) collective-permute-start(bf16[256,8192]{1,0:T(8,128)(2,1)} %shard_map.92), channel_id=1, source_target_pairs={{0,2},{1,3},{2,0},{3,1},{4,6},{5,7},{6,4},{7,5}} | collective-permute-start | bytes 12582920 | tf_op jit(solution)/shard_map/ppermute | solution.py:317
  313.6 474.2 %all-gather.19.cloned.1.call-start = ((), (), s32[]{:S(2)}) async-start(), calls=%async_computation.10 | async-start | bytes 12582912 | tf_op jit(solution)/shard_map/all_gather | solution.py:320
  313.6 89.9 %collective-permute-start.2 = (bf16[256,8192]{1,0:T(8,128)(2,1)}, bf16[256,8192]{1,0:T(8,128)(2,1)}, u32[]{:S(2)}, u32[]{:S(2)}) collective-permute-start(bf16[256,8192]{1,0:T(8,128)(2,1)} %get-tuple-element.34), channel_id=1, source_target_pairs={{0,2},{1,3},{2,0},{3,1},{4,6},{5,7},{6,4},{7,5}} | collective-permute-start | bytes 12582920 | tf_op jit(solution)/shard_map/ppermute | solution.py:317
  403.5 788.7 %reduce-scatter.11.cloned.1.call-start = ((), (), s32[]{:S(2)}) async-start(), calls=%async_computation.13 | async-start | bytes 20971520 | tf_op jit(solution)/shard_map/reduce_scatter | solution.py:323
  660.0 546.2 %reduce-scatter.9.cloned.1.call-start = ((), (), s32[]{:S(2)}) async-start(), calls=%async_computation.11 | async-start | bytes 20971520 | tf_op jit(solution)/shard_map/reduce_scatter | solution.py:323
  918.6 302.2 %reduce-scatter.7.cloned.1.call-start = ((), (), s32[]{:S(2)}) async-start(), calls=%async_computation.9 | async-start | bytes 20971520 | tf_op jit(solution)/shard_map/reduce_scatter | solution.py:323
  961.2 322.0 %reduce-scatter.5.cloned.1.call-start = ((), (), s32[]{:S(2)}) async-start(), calls=%async_computation.6 | async-start | bytes 20971520 | tf_op jit(solution)/shard_map/reduce_scatter | solution.py:323
  1206.2 13.8 %copy-start = (f32[1,8192]{1,0:T(1,128)S(1)}, f32[1,8192]{1,0:T(1,128)}, u32[]{:S(2)}) copy-start(f32[1,8192]{1,0:T(1,128)} %get-tuple-element.27) | copy-start | bytes 98308
Sparse Core Ops, SparseCore 0:
  17.2 19.8 all-gather.14
  39.2 18.2 all-gather.24
  121.6 18.3 all-gather.16
  213.5 18.1 all-gather.20
  233.0 18.2 all-gather.22
  253.2 18.2 all-gather.10
  313.7 18.0 all-gather.12
  403.7 17.8 all-gather.18
  660.1 120.1 reduce-scatter.10
  918.8 119.9 reduce-scatter.8
  1041.3 119.4 reduce-scatter.6
  1163.2 120.0 reduce-scatter.4

commit v3 on v2

--- a/solution.py
+++ b/solution.py
@@ -126,9 +126,13 @@
         q_rot = rope(q_in, cos_ref[rows, :], sin_ref[rows, :]).astype(jnp.bfloat16)
         return dot32(k_scr[:(i + 1) * QBLK, :], q_rot, NT)
 
-    for i in range(seq // QBLK):
+    blocks = seq // QBLK
+    ahead = scores(0)
+    for i in range(blocks):
         rows = slice(i * QBLK, (i + 1) * QBLK)
-        s = masked_tail(scores(i) * scale, -1e30)
+        s = masked_tail(ahead * scale, -1e30)
+        if i + 1 < blocks:
+            ahead = scores(i + 1)
         top = jnp.max(s, axis=0, keepdims=True)
         e = jnp.exp2(s - top)
         total = jnp.sum(e, axis=0, keepdims=True)
@@ -163,16 +167,27 @@
 
     col = pl.ds(pl.multiple_of(head * dim, dim), dim)
     scale = dim ** -0.5
-    for i in range(seq // QBLK):
+    blocks = seq // QBLK
+
+    def load(i):
         rows = slice(i * QBLK, (i + 1) * QBLK)
         kend = (i + 1) * QBLK
         q_raw = qkv_scr[rows, col].astype(jnp.float32)
         q_rot = rope(clip(q_raw), cos_ref[rows, :], sin_ref[rows, :]).astype(jnp.bfloat16)
+        s = dot32(k_scr[:kend, :], q_rot, NT)
+        dp = dot32(v_scr[:kend, :], do_scr[rows, col], NT)
+        return rows, kend, q_raw, q_rot, s, dp
+
+    ahead = load(0)
+    for i in range(blocks):
+        rows, kend, q_raw, q_rot, s, dp = ahead
         d_o = do_scr[rows, col]
-        s = dot32(k_scr[:kend, :], q_rot, NT) * (LOG2E * scale) - lse_ref[0, pl.ds(head, 1), rows]
+        if i + 1 < blocks:
+            ahead = load(i + 1)
+        s = s * (LOG2E * scale) - lse_ref[0, pl.ds(head, 1), rows]
         p = jnp.exp2(masked_tail(s, -1e30))
         dv_scr[:kend, :] += dot32(p.astype(jnp.bfloat16), d_o, NN)
-        dp = dot32(v_scr[:kend, :], d_o, NT).astype(jnp.bfloat16).astype(jnp.float32)
+        dp = dp.astype(jnp.bfloat16).astype(jnp.float32)
         t = p * dp
         delta = jnp.sum(t, axis=0, keepdims=True)
         ds = (t - p * delta).astype(jnp.bfloat16)

time: 1300 us -> 1260 us (0.969)
  Pallas kernels: 357 us -> 315 us
    pallas_call x2, Pallas kernels: 109 us -> 85.3 us  [attn_bwd(): pl.pallas_call(functools.partial(attn_bwd_kernel, groups, dim), grid=(kv_...]
    pallas_call x2, Pallas kernels: 82 us -> 63.3 us  [attn_fwd(): pl.pallas_call(functools.partial(attn_fwd_kernel, groups, dim), grid=(kv_...]
  transfers between devices with their start and end apart: 16 -> 16, of which waited for: 5 -> 5; matrix products, arithmetic and copies ran while one was open for 39% -> 40% of each run, Pallas kernels for 26% -> 24%
where the time goes in v3:
time: 1260 us; the launch traced here: 1250 us
  matrix products  489 us (39%)
  waiting for transfers between devices  399 us (32%)
  Pallas kernels  315 us (25%)
  between operations  14.5 us (1%)
  blocking collectives  12.7 us (1%)
    dot_general x13, matrix products, ein(): jnp.einsum(spec, a, b, preferred_element_type=jnp.float32)  489 us
    ppermute x4, waiting for transfers between devices, across(): return lax.ppermute(v, 'tp', [(d, (d + 2) % 4) for d in range(4)])  355 us
    pallas_call x1, Pallas kernels, wqkv_grad_call(): pl.pallas_call(functools.partial(wqkv_grad_kernel, len(h_pieces)), grid=(...  110 us
    pallas_call x2, Pallas kernels, attn_bwd(): pl.pallas_call(functools.partial(attn_bwd_kernel, groups, dim), grid=(kv_...  85.3 us
    pallas_call x2, Pallas kernels, attn_fwd(): pl.pallas_call(functools.partial(attn_fwd_kernel, groups, dim), grid=(kv_...  63.3 us
    pallas_call x6, Pallas kernels, row_call(): pl.pallas_call(body, grid=(tokens // rows,), in_specs=specs, out_specs=[o...  56.9 us
    reduce_scatter x4, waiting for transfers between devices, scatter(): return lax.psum_scatter(v, 'tp', scatter_dimension=0, tiled=True)  43.1 us
  transfers between devices with their start and end apart: 16, of which 5 were waited for; matrix products, arithmetic and copies ran while one was open for 40% of the time, Pallas kernels for 24%

profile of v3, /device:TPU:0, one launch (start us, length us, event | category | flops | bytes accessed | tf_op | source)
XLA Modules:
  0.0 1254.2 jit_solution(4478628945478848413)
XLA Ops:
  7.2 1.3 reshape.24.gain_ref
  8.5 8.5 shard_map.93
  17.0 0.0 all-gather.25.cloned.1.call-start
  17.1 9.5 slice_bitcast_fusion
  26.6 0.0 all-gather.17.cloned.1.call-start
  26.6 4.3 collective-permute-start.1
  30.9 90.6 %collective-permute-done.1 = bf16[256,8192]{1,0:T(8,128)(2,1)} collective-permute-done((bf16[256,8192]{1,0:T(8,128)(2,1)}, bf16[256,8192]{1,0:T(8,128)(2,1)}, u32[]{:S(2)}, u32[]{:S(2)}) %collective-permute-start.1) | collective-permute-done | bytes 4194336 | tf_op jit(solution)/shard_map/ppermute | solution.py:332
  121.6 1.8 collective-permute-start.3
  123.3 90.0 %collective-permute-done.3 = bf16[256,8192]{1,0:T(8,128)(2,1)} collective-permute-done((bf16[256,8192]{1,0:T(8,128)(2,1)}, bf16[256,8192]{1,0:T(8,128)(2,1)}, u32[]{:S(2)}, u32[]{:S(2)}) %collective-permute-start.3) | collective-permute-done | bytes 4194336 | tf_op jit(solution)/shard_map/ppermute | solution.py:332
  213.4 0.5 all-gather.23.cloned.1.call-update
  213.9 0.0 all-gather.11.cloned.1.call-start
  214.0 8.7 shard_map.92
  222.7 0.0 all-gather.13.cloned.1.call-start
  222.8 1.5 collective-permute-start
  224.2 89.3 %collective-permute-done = bf16[256,8192]{1,0:T(8,128)(2,1)} collective-permute-done((bf16[256,8192]{1,0:T(8,128)(2,1)}, bf16[256,8192]{1,0:T(8,128)(2,1)}, u32[]{:S(2)}, u32[]{:S(2)}) %collective-permute-start) | collective-permute-done | bytes 4194336 | tf_op jit(solution)/shard_map/ppermute | solution.py:332
  313.6 1.4 collective-permute-start.2
  315.0 2.0 fusion.70
  317.0 1.3 pad_maximum_fusion
  318.3 85.2 %collective-permute-done.2 = bf16[256,8192]{1,0:T(8,128)(2,1)} collective-permute-done((bf16[256,8192]{1,0:T(8,128)(2,1)}, bf16[256,8192]{1,0:T(8,128)(2,1)}, u32[]{:S(2)}, u32[]{:S(2)}) %collective-permute-start.2) | collective-permute-done | bytes 4194336 | tf_op jit(solution)/shard_map/ppermute | solution.py:332
  403.5 0.2 reduce-scatter.11.cloned.1.call-start
  403.8 30.6 %fusion.53.own_ref = bf16[2,512,1280]{2,1,0:T(8,128)(2,1)} fusion(bf16[8192,2,1280]{2,1,0:T(2,128)(2,1)} %param.7, bf16[512,8192]{1,0:T(8,128)(2,1)} %all-gather.15.cloned.1.call-done.refs_0_), kind=kOutput, calls=%fused_computation.35 | convolution fusion | flops 21476147200 | bytes 52953088 | tf_op jit(solution)/shard_map/sd,dnc->nsc/dot_general | solution.py:319
  434.4 24.7 %convolution_convert_fusion.3.do_own_ref = bf16[512,2048]{1,0:T(8,128)(2,1)} fusion(bf16[2048,8192]{1,0:T(8,128)(2,1)} %param.8, bf16[1,512,8192]{2,1,0:T(8,128)(2,1)} %all-gather.25.cloned.1.call-done), kind=kOutput, calls=%fused_computation.39 | convolution fusion | flops 17180917760 | bytes 44040192 | tf_op jit(solution)/shard_map/sd,kd->sk/dot_general | solution.py:319
  459.1 29.3 %fusion.48.oth_ref = bf16[2,512,1280]{2,1,0:T(8,128)(2,1)} fusion(bf16[8192,2,1280]{2,1,0:T(2,128)(2,1)} %param.7, bf16[512,8192]{1,0:T(8,128)(2,1)} %all-gather.17.cloned.1.call-done.refs_1_), kind=kOutput, calls=%fused_computation.34 | convolution fusion | flops 21476147200 | bytes 52953088 | tf_op jit(solution)/shard_map/sd,dnc->nsc/dot_general | solution.py:319
  488.4 31.7 %attn_fwd.3 = (bf16[1024,2048]{1,0:T(8,128)(2,1)}, bf16[1024,2048]{1,0:T(8,128)(2,1)}, f32[2,8,1024]{2,1,0:T(8,128)}) custom-call(s32[1]{0:T(128)} %bitcast.chip_ref, bf16[2,512,1280]{2,1,0:T(8,128)(2,1)} %fusion.53.own_ref, bf16[2,512,1280]{2,1,0:T(8,128)(2,1)} %fusion.48.oth_ref, f32[1024,128]{1,0:T(8,128)} %get-tuple-element.40.cos_ref, ...), custom_call_target="tpu_custom_call" | custom-call | flops 17179869184 | bytes 18874368 | tf_op jit(solution)/shard_map/attn_fwd/pallas_call | solution.py:230
  520.2 24.8 %convolution_convert_fusion.2.do_oth_ref = bf16[512,2048]{1,0:T(8,128)(2,1)} fusion(bf16[512,8192]{1,0:T(8,128)(2,1)} %all-gather.21.cloned.1.call-done, bf16[2048,8192]{1,0:T(8,128)(2,1)} %param.8), kind=kOutput, calls=%fused_computation.38 | convolution fusion | flops 17180917760 | bytes 44040192 | tf_op jit(solution)/shard_map/sd,kd->sk/dot_general | solution.py:319
  544.9 42.7 %attn_bwd.3 = (bf16[2,1024,1280]{2,1,0:T(8,128)(2,1)}, bf16[2,1024,1280]{2,1,0:T(8,128)(2,1)}) custom-call(s32[1]{0:T(128)} %bitcast.chip_ref, bf16[2,512,1280]{2,1,0:T(8,128)(2,1)} %fusion.53.own_ref, bf16[2,512,1280]{2,1,0:T(8,128)(2,1)} %fusion.48.oth_ref, bf16[512,2048]{1,0:T(8,128)(2,1)} %convolution_convert_fusion.3.do_own_ref, ...), custom_call_target="tpu_custom_call" | custom-call | flops 34359738368 | bytes 18874368 | tf_op jit(solution)/shard_map/attn_bwd/pallas_call | solution.py:252
  587.6 51.3 %bitcast_convert_fusion = bf16[1024,8192]{1,0:T(8,128)(2,1)} fusion(bf16[2,1024,1280]{2,1,0:T(8,128)(2,1)} %get-tuple-element.24, bf16[8192,2,1280]{2,1,0:T(2,128)(2,1)} %param.7), kind=kOutput, calls=%fused_computation.8 | convolution fusion | flops 42958061568 | bytes 63963136 | tf_op jit(solution)/shard_map/nsc,dnc->sd/dot_general | solution.py:319
  638.9 0.0 reduce-scatter.9.cloned.1.call-start
  639.0 28.3 %convolution_convert_fusion.5.do_own_ref = bf16[512,2048]{1,0:T(8,128)(2,1)} fusion(bf16[2048,8192]{1,0:T(8,128)(2,1)} %param.8, bf16[1,512,8192]{2,1,0:T(8,128)(2,1)} %all-gather.23.cloned.1.call-done), kind=kOutput, calls=%fused_computation.41 | convolution fusion | flops 17180917760 | bytes 44040192 | tf_op jit(solution)/shard_map/sd,kd->sk/dot_general | solution.py:319
  667.2 29.4 %fusion.63.own_ref = bf16[2,512,1280]{2,1,0:T(8,128)(2,1)} fusion(bf16[8192,2,1280]{2,1,0:T(2,128)(2,1)} %param.7, bf16[512,8192]{1,0:T(8,128)(2,1)} %all-gather.11.cloned.1.call-done.refs_2_), kind=kOutput, calls=%fused_computation.37 | convolution fusion | flops 21476147200 | bytes 52953088 | tf_op jit(solution)/shard_map/sd,dnc->nsc/dot_general | solution.py:319
  696.7 29.6 %fusion.58.oth_ref = bf16[2,512,1280]{2,1,0:T(8,128)(2,1)} fusion(bf16[8192,2,1280]{2,1,0:T(2,128)(2,1)} %param.7, bf16[512,8192]{1,0:T(8,128)(2,1)} %all-gather.13.cloned.1.call-done.refs_3_), kind=kOutput, calls=%fused_computation.36 | convolution fusion | flops 21476147200 | bytes 52953088 | tf_op jit(solution)/shard_map/sd,dnc->nsc/dot_general | solution.py:319
  726.3 31.6 %attn_fwd.2 = (bf16[1024,2048]{1,0:T(8,128)(2,1)}, bf16[1024,2048]{1,0:T(8,128)(2,1)}, f32[2,8,1024]{2,1,0:T(8,128)}) custom-call(s32[1]{0:T(128)} %bitcast.chip_ref, bf16[2,512,1280]{2,1,0:T(8,128)(2,1)} %fusion.63.own_ref, bf16[2,512,1280]{2,1,0:T(8,128)(2,1)} %fusion.58.oth_ref, f32[1024,128]{1,0:T(8,128)} %get-tuple-element.40.cos_ref, ...), custom_call_target="tpu_custom_call" | custom-call | flops 17179869184 | bytes 18874368 | tf_op jit(solution)/shard_map/attn_fwd/pallas_call | solution.py:230
  757.9 24.8 %convolution_convert_fusion.4.do_oth_ref = bf16[512,2048]{1,0:T(8,128)(2,1)} fusion(bf16[512,8192]{1,0:T(8,128)(2,1)} %all-gather.19.cloned.1.call-done, bf16[2048,8192]{1,0:T(8,128)(2,1)} %param.8), kind=kOutput, calls=%fused_computation.40 | convolution fusion | flops 17180917760 | bytes 44040192 | tf_op jit(solution)/shard_map/sd,kd->sk/dot_general | solution.py:319
  782.7 42.7 %attn_bwd.2 = (bf16[2,1024,1280]{2,1,0:T(8,128)(2,1)}, bf16[2,1024,1280]{2,1,0:T(8,128)(2,1)}) custom-call(s32[1]{0:T(128)} %bitcast.chip_ref, bf16[2,512,1280]{2,1,0:T(8,128)(2,1)} %fusion.63.own_ref, bf16[2,512,1280]{2,1,0:T(8,128)(2,1)} %fusion.58.oth_ref, bf16[512,2048]{1,0:T(8,128)(2,1)} %convolution_convert_fusion.5.do_own_ref, ...), custom_call_target="tpu_custom_call" | custom-call | flops 34359738368 | bytes 18874368 | tf_op jit(solution)/shard_map/attn_bwd/pallas_call | solution.py:252
  825.4 51.5 %bitcast_convert_fusion.1 = bf16[1024,8192]{1,0:T(8,128)(2,1)} fusion(bf16[2,1024,1280]{2,1,0:T(8,128)(2,1)} %get-tuple-element.22, bf16[8192,2,1280]{2,1,0:T(2,128)(2,1)} %param.7), kind=kOutput, calls=%fused_computation.9 | convolution fusion | flops 42958061568 | bytes 63963136 | tf_op jit(solution)/shard_map/nsc,dnc->sd/dot_general | solution.py:319
  876.9 0.0 reduce-scatter.7.cloned.1.call-start
  876.9 42.5 %convolution_convert_fusion = bf16[1024,8192]{1,0:T(8,128)(2,1)} fusion(bf16[1024,2048]{1,0:T(8,128)(2,1)} %get-tuple-element.20, bf16[2048,8192]{1,0:T(8,128)(2,1)} %param.8), kind=kOutput, calls=%fused_computation.21 | convolution fusion | flops 34368126976 | bytes 54525952 | tf_op jit(solution)/shard_map/sk,kd->sd/dot_general | solution.py:319
  919.5 0.0 reduce-scatter.5.cloned.1.call-start
  919.5 42.4 %convolution_convert_fusion.1 = bf16[1024,8192]{1,0:T(8,128)(2,1)} fusion(bf16[1024,2048]{1,0:T(8,128)(2,1)} %get-tuple-element.19, bf16[2048,8192]{1,0:T(8,128)(2,1)} %param.8), kind=kOutput, calls=%fused_computation.22 | convolution fusion | flops 34368126976 | bytes 54525952 | tf_op jit(solution)/shard_map/sk,kd->sd/dot_general | solution.py:319
  962.0 109.6 %wqkv_grad.1 = bf16[8192,2,1280]{2,1,0:T(2,128)(2,1)} custom-call(bf16[512,8192]{1,0:T(8,128)(2,1)} %all-gather.15.cloned.1.call-done.refs_0_, bf16[512,8192]{1,0:T(8,128)(2,1)} %all-gather.17.cloned.1.call-done.refs_1_, bf16[512,8192]{1,0:T(8,128)(2,1)} %all-gather.11.cloned.1.call-done.refs_2_, bf16[512,8192]{1,0:T(8,128)(2,1)} %all-gather.13.cloned.1.call-done.refs_3_, ...), custom_call_target="tpu_custom_call" | custom-call | flops 85899345920 | bytes 83886080 | tf_op jit(solution)/shard_map/wqkv_grad/pallas_call | solution.py:283
  1071.6 79.3 %fusion.8 = bf16[2048,8192]{1,0:T(8,128)(2,1)} fusion(bf16[512,8192]{1,0:T(8,128)(2,1)} %all-gather.19.cloned.1.call-done, bf16[512,8192]{1,0:T(8,128)(2,1)} %bitcast.66, bf16[512,8192]{1,0:T(8,128)(2,1)} %all-gather.21.cloned.1.call-done, bf16[512,8192]{1,0:T(8,128)(2,1)} %bitcast.65, bf16[1024,2048]{1,0:T(8,128)(2,1)} %get-tuple-element.32, ...), kind=kOutput, calls=%fused_computation.10 | convolution fusion | flops 68887248896 | bytes 75497472 | tf_op jit(solution)/shard_map/sk,sd->kd/dot_general | solution.py:319
  1150.9 14.0 %shard_map.96 = (bf16[2,256,8192]{2,1,0:T(8,128)(2,1)}, f32[1,8192]{1,0:T(1,128)}) custom-call(bf16[256,8192]{1,0:T(8,128)(2,1)} %reduce-scatter.11.cloned.1.call-done.dh_ref, bf16[2,256,8192]{2,1,0:T(8,128)(2,1)} %x_ref.11, bf16[2,256,8192]{2,1,0:T(8,128)(2,1)} %dy_ref.3, bf16[1,8192]{1,0:T(2,128)(2,1)} %reshape.24.gain_ref), custom_call_target="tpu_custom_call" | custom-call | flops 83886080 | bytes 16777216 | tf_op jit(solution)/shard_map/pallas_call | solution.py:309
  1164.9 13.7 %shard_map.97 = (bf16[2,256,8192]{2,1,0:T(8,128)(2,1)}, f32[1,8192]{1,0:T(1,128)}) custom-call(bf16[256,8192]{1,0:T(8,128)(2,1)} %reduce-scatter.9.cloned.1.call-done.dh_ref, bf16[2,256,8192]{2,1,0:T(8,128)(2,1)} %x_ref.11, bf16[2,256,8192]{2,1,0:T(8,128)(2,1)} %dy_ref.3, bf16[1,8192]{1,0:T(2,128)(2,1)} %reshape.24.gain_ref, ...), custom_call_target="tpu_custom_call", output_to_operand_aliasing={{0}: (4, {})} | custom-call | flops 83886080 | bytes 20971520 | tf_op jit(solution)/shard_map/pallas_call | solution.py:309
  1178.6 0.8 add.17
  1179.4 6.0 shard_map.94.refs_0_
  1185.5 12.7 %psum.7 = bf16[8192]{0:T(1024)(128)(2,1)} all-reduce(f32[8192]{0:T(1024)S(1)} %bitcast.64), channel_id=1, replica_groups=mesh['dp'=2,'tp'=4] {'tp'}, use_global_device_ids=true, to_apply=%region_4.5 | all-reduce | flops 8192 | bytes 49152 | tf_op jit(solution)/shard_map/psum | solution.py:372
  1198.1 43.1 %reduce-scatter.5.cloned.1.call-done.o_ref = bf16[256,8192]{1,0:T(8,128)(2,1)} async-done(((bf16[1024,8192]{1,0:T(8,128)(2,1)}), bf16[256,8192]{1,0:T(8,128)(2,1)}) %reduce-scatter.5.cloned.1.call-update) | async-done | bytes 4194320 | tf_op jit(solution)/shard_map/reduce_scatter | solution.py:338
  1241.2 6.0 shard_map.95
  (29 shorter events, 0.4 us)
Async XLA Ops:
  7.2 396.6 %all-gather.15.cloned.1.call-start = ((), (), s32[]{:S(2)}) async-start(), calls=%async_computation.7 | async-start | bytes 12582912 | tf_op jit(solution)/shard_map/all_gather | solution.py:335
  17.0 417.3 %all-gather.25.cloned.1.call-start = ((), (), s32[]{:S(2)}) async-start(), calls=%async_computation.15 | async-start | bytes 12582912 | tf_op jit(solution)/shard_map/all_gather | solution.py:335
  26.6 432.5 %all-gather.17.cloned.1.call-start = ((), (), s32[]{:S(2)}) async-start(), calls=%async_computation.8 | async-start | bytes 12582912 | tf_op jit(solution)/shard_map/all_gather | solution.py:335
  26.6 94.9 %collective-permute-start.1 = (bf16[256,8192]{1,0:T(8,128)(2,1)}, bf16[256,8192]{1,0:T(8,128)(2,1)}, u32[]{:S(2)}, u32[]{:S(2)}) collective-permute-start(bf16[256,8192]{1,0:T(8,128)(2,1)} %shard_map.93), channel_id=1, source_target_pairs={{0,2},{1,3},{2,0},{3,1},{4,6},{5,7},{6,4},{7,5}} | collective-permute-start | bytes 12582920 | tf_op jit(solution)/shard_map/ppermute | solution.py:332
  121.5 398.6 %all-gather.21.cloned.1.call-start = ((), (), s32[]{:S(2)}) async-start(), calls=%async_computation.12 | async-start | bytes 12582912 | tf_op jit(solution)/shard_map/all_gather | solution.py:335
  121.6 91.7 %collective-permute-start.3 = (bf16[256,8192]{1,0:T(8,128)(2,1)}, bf16[256,8192]{1,0:T(8,128)(2,1)}, u32[]{:S(2)}, u32[]{:S(2)}) collective-permute-start(bf16[256,8192]{1,0:T(8,128)(2,1)} %get-tuple-element.33), channel_id=1, source_target_pairs={{0,2},{1,3},{2,0},{3,1},{4,6},{5,7},{6,4},{7,5}} | collective-permute-start | bytes 12582920 | tf_op jit(solution)/shard_map/ppermute | solution.py:332
  213.3 425.6 %all-gather.23.cloned.1.call-start = ((), (), s32[]{:S(2)}) async-start(), calls=%async_computation.14 | async-start | bytes 12582912 | tf_op jit(solution)/shard_map/all_gather | solution.py:335
  213.9 453.3 %all-gather.11.cloned.1.call-start = ((), (), s32[]{:S(2)}) async-start(), calls=%async_computation.4 | async-start | bytes 12582912 | tf_op jit(solution)/shard_map/all_gather | solution.py:335
  222.7 473.9 %all-gather.13.cloned.1.call-start = ((), (), s32[]{:S(2)}) async-start(), calls=%async_computation.5 | async-start | bytes 12582912 | tf_op jit(solution)/shard_map/all_gather | solution.py:335
  222.8 90.8 %collective-permute-start = (bf16[256,8192]{1,0:T(8,128)(2,1)}, bf16[256,8192]{1,0:T(8,128)(2,1)}, u32[]{:S(2)}, u32[]{:S(2)}) collective-permute-start(bf16[256,8192]{1,0:T(8,128)(2,1)} %shard_map.92), channel_id=1, source_target_pairs={{0,2},{1,3},{2,0},{3,1},{4,6},{5,7},{6,4},{7,5}} | collective-permute-start | bytes 12582920 | tf_op jit(solution)/shard_map/ppermute | solution.py:332
  313.6 444.3 %all-gather.19.cloned.1.call-start = ((), (), s32[]{:S(2)}) async-start(), calls=%async_computation.10 | async-start | bytes 12582912 | tf_op jit(solution)/shard_map/all_gather | solution.py:335
  313.6 89.9 %collective-permute-start.2 = (bf16[256,8192]{1,0:T(8,128)(2,1)}, bf16[256,8192]{1,0:T(8,128)(2,1)}, u32[]{:S(2)}, u32[]{:S(2)}) collective-permute-start(bf16[256,8192]{1,0:T(8,128)(2,1)} %get-tuple-element.34), channel_id=1, source_target_pairs={{0,2},{1,3},{2,0},{3,1},{4,6},{5,7},{6,4},{7,5}} | collective-permute-start | bytes 12582920 | tf_op jit(solution)/shard_map/ppermute | solution.py:332
  403.5 747.4 %reduce-scatter.11.cloned.1.call-start = ((), (), s32[]{:S(2)}) async-start(), calls=%async_computation.13 | async-start | bytes 20971520 | tf_op jit(solution)/shard_map/reduce_scatter | solution.py:338
  638.9 526.0 %reduce-scatter.9.cloned.1.call-start = ((), (), s32[]{:S(2)}) async-start(), calls=%async_computation.11 | async-start | bytes 20971520 | tf_op jit(solution)/shard_map/reduce_scatter | solution.py:338
  876.9 302.5 %reduce-scatter.7.cloned.1.call-start = ((), (), s32[]{:S(2)}) async-start(), calls=%async_computation.9 | async-start | bytes 20971520 | tf_op jit(solution)/shard_map/reduce_scatter | solution.py:338
  919.5 321.7 %reduce-scatter.5.cloned.1.call-start = ((), (), s32[]{:S(2)}) async-start(), calls=%async_computation.6 | async-start | bytes 20971520 | tf_op jit(solution)/shard_map/reduce_scatter | solution.py:338
  1164.9 13.7 %copy-start = (f32[1,8192]{1,0:T(1,128)S(1)}, f32[1,8192]{1,0:T(1,128)}, u32[]{:S(2)}) copy-start(f32[1,8192]{1,0:T(1,128)} %get-tuple-element.27) | copy-start | bytes 98308
Sparse Core Ops, SparseCore 0:
  17.2 19.8 all-gather.14
  39.2 18.2 all-gather.24
  121.6 18.3 all-gather.16
  213.5 18.1 all-gather.20
  233.0 18.2 all-gather.22
  253.2 18.2 all-gather.10
  313.7 18.0 all-gather.12
  403.7 17.8 all-gather.18
  639.0 120.1 reduce-scatter.10
  877.0 119.6 reduce-scatter.8
  999.2 119.4 reduce-scatter.6
  1121.2 119.9 reduce-scatter.4
